TPU v7x, 32 devices: a whole 2x2x4 slice. The times are simulated.
32 devices in a mesh: fsdp: 4 (over y, x), seq: 4 (over z), mlp: 2 (over core).
Axes of the slice: x: 2, y: 2, z: 4, core: 2. Of those that a mesh axis runs over, the one named last changes fastest.
Arguments:
- block_in: float32 [8, 1024, 2304], P(('fsdp', 'mlp'), 'seq'), may hold values from -6 to 6
- cotangent: float32 [8, 1024, 2304], P(('fsdp', 'mlp'), 'seq'), may hold values from -6 to 6
- attention_matrix: float32 [2304, 6144], P(('fsdp', 'seq', 'mlp')), may hold values from -0.25 to 0.25
- attention_first_moment: float32 [2304, 6144], P(('fsdp', 'seq', 'mlp')), may hold values from -48 to 48
- attention_second_moment: float32 [2304, 6144], P(('fsdp', 'seq', 'mlp')), may hold values from 5 to 500
- mlp_weight: float32 [3, 2304, 9216], P(None, 'fsdp', ('seq', 'mlp')), may hold values from -0.125 to 0.125
- first_mlp: float32 [3, 2304, 9216], P(None, 'fsdp', ('seq', 'mlp')), may hold values from -48 to 48
- second_mlp: float32 [3, 2304, 9216], P(None, 'fsdp', ('seq', 'mlp')), may hold values from 5 to 500
- norm_weight: float32 [4, 2304], P(None, ('fsdp', 'seq', 'mlp')), may hold values from -0.3 to 0.3
- first_norm: float32 [4, 2304], P(None, ('fsdp', 'seq', 'mlp')), may hold values from -48 to 48
- second_norm: float32 [4, 2304], P(None, ('fsdp', 'seq', 'mlp')), may hold values from 5 to 500
Outputs:
- block_out: float32 [8, 1024, 2304], P(('fsdp', 'mlp'), 'seq')
- input_grad: float32 [8, 1024, 2304], P(('fsdp', 'mlp'), 'seq')
- attn_grad: float32 [2304, 6144], P(('fsdp', 'seq', 'mlp'))
- attn_new: float32 [2304, 6144], P(('fsdp', 'seq', 'mlp'))
- first_attn_new: float32 [2304, 6144], P(('fsdp', 'seq', 'mlp'))
- second_attn_new: float32 [2304, 6144], P(('fsdp', 'seq', 'mlp'))
- mlp_grad: float32 [3, 2304, 9216], P(None, 'fsdp', ('seq', 'mlp'))
- mlp_new: float32 [3, 2304, 9216], P(None, 'fsdp', ('seq', 'mlp'))
- first_mlp_new: float32 [3, 2304, 9216], P(None, 'fsdp', ('seq', 'mlp'))
- second_mlp_new: float32 [3, 2304, 9216], P(None, 'fsdp', ('seq', 'mlp'))
- norm_grad: float32 [4, 2304], P(None, ('fsdp', 'seq', 'mlp'))
- norm_new: float32 [4, 2304], P(None, ('fsdp', 'seq', 'mlp'))
- first_norm_new: float32 [4, 2304], P(None, ('fsdp', 'seq', 'mlp'))
- second_norm_new: float32 [4, 2304], P(None, ('fsdp', 'seq', 'mlp'))
All inputs are finite; a program needn't handle non-finite values.
Results may differ from a plain program's by a relative error of at most 0.03.
Values may be sent and summed in bfloat16 or wider, within the bound.
A program may use at most 384 MiB of HBM per device.

v0:
```python
import jax
import jax.numpy as jnp
from jax import lax
from jax.sharding import PartitionSpec as P

QUERY_HEADS = 8
KEY_VALUE_HEADS = 4
HEAD_SIZE = 256


softcap = 50.0
norm_eps = 1e-06
beta_one = 0.9
beta_two = 0.95
adam_eps = 1e-08
learn_rate = 0.01
decay_rate = 0.1
step_count = 2


def scale_rows(values):
    return lax.rsqrt(jnp.mean(values * values, axis=-1, keepdims=True) + norm_eps)


def norm_back(values, inverse, factor, upstream):
    normed = values * inverse
    scaled = upstream * factor
    inner_mean = jnp.mean(scaled * normed, axis=-1, keepdims=True)
    return (inverse * (scaled - normed * inner_mean), jnp.sum(upstream * normed, axis=0))


def gelu_tanh(values):
    return jax.nn.gelu(values, approximate=True)


def adam_update(weight, gradient, first_moment, second_moment, decay_factor):
    first_new = beta_one * first_moment + (1.0 - beta_one) * gradient
    second_new = beta_two * second_moment + (1.0 - beta_two) * gradient * gradient
    first_hat = first_new / (1.0 - beta_one**step_count)
    second_hat = second_new / (1.0 - beta_two**step_count)
    weight_new = weight - learn_rate * (
        first_hat / (jnp.sqrt(second_hat) + adam_eps) + decay_factor * weight
    )
    return (weight_new, first_new, second_new)


def forward_scores(queries, key_head_rows, row_start):
    head_width = queries.shape[3]
    raw_scores = jnp.einsum(
        "sqlc,sklc->slqk", queries, key_head_rows, preferred_element_type=jnp.float32
    ) * head_width ** (-0.5)
    capped = softcap * jnp.tanh(raw_scores / softcap)
    shape_pair = (queries.shape[1], key_head_rows.shape[1])
    row_index = row_start + lax.broadcasted_iota(jnp.int32, shape_pair, 0)
    col_index = lax.broadcasted_iota(jnp.int32, shape_pair, 1)
    return (capped, col_index <= row_index)


def attend(queries, key_head_rows, value_head_rows, block_rows):
    sequence_count, length, head_count, head_width = queries.shape

    def one_block(block_index, carry_state):
        row_start = block_index * block_rows
        query_part = lax.dynamic_slice_in_dim(queries, row_start, block_rows, 1)
        capped, causal = forward_scores(query_part, key_head_rows, row_start)
        logsum = jnp.log(jnp.sum(jnp.where(causal, jnp.exp(capped), 0.0), axis=-1))
        prob_full = jnp.where(causal, jnp.exp(capped - logsum[..., None]), 0.0)
        prob_bf = prob_full.astype(jnp.bfloat16)
        mixed_part = jnp.einsum(
            "slqk,sklc->sqlc", prob_bf, value_head_rows, preferred_element_type=jnp.float32
        ).astype(jnp.bfloat16)
        outputs = lax.dynamic_update_slice_in_dim(carry_state[0], mixed_part, row_start, 1)
        totals = lax.dynamic_update_slice_in_dim(carry_state[1], logsum, row_start, 2)
        return (outputs, totals)

    start_state = (
        jnp.zeros(queries.shape, jnp.bfloat16),
        jnp.zeros((sequence_count, head_count, length), jnp.float32),
    )
    end_state = lax.fori_loop(0, length // block_rows, one_block, start_state)
    return (end_state[0], end_state[1], tuple(end_state[2:]))


def attend_back(queries, key_head_rows, value_head_rows, outputs, totals, upstream, block_rows):
    sequence_count, length, head_count, head_width = queries.shape
    row_inner = jnp.sum(upstream.astype(jnp.float32) * outputs.astype(jnp.float32), axis=-1)

    def one_block(block_index, carry_state):
        dquery, dkey_acc, dvalue_acc = carry_state
        row_start = block_index * block_rows
        query_part = lax.dynamic_slice_in_dim(queries, row_start, block_rows, 1)
        grad_part = lax.dynamic_slice_in_dim(upstream, row_start, block_rows, 1)
        inner_part = lax.dynamic_slice_in_dim(row_inner, row_start, block_rows, 1)
        logsum = lax.dynamic_slice_in_dim(totals, row_start, block_rows, 2)
        capped, causal = forward_scores(query_part, key_head_rows, row_start)
        prob_full = jnp.where(causal, jnp.exp(capped - logsum[..., None]), 0.0)
        dprob = jnp.einsum(
            "sqlc,sklc->slqk", grad_part, value_head_rows, preferred_element_type=jnp.float32
        )
        dcapped = prob_full * (dprob - jnp.transpose(inner_part, (0, 2, 1))[..., None])
        dscore = (
            dcapped * (1.0 - capped / softcap * (capped / softcap)) * head_width ** (-0.5)
        ).astype(jnp.bfloat16)
        dquery_part = jnp.einsum(
            "slqk,sklc->sqlc", dscore, key_head_rows, preferred_element_type=jnp.float32
        ).astype(jnp.bfloat16)
        dquery = lax.dynamic_update_slice_in_dim(dquery, dquery_part, row_start, 1)
        dkey_acc = dkey_acc + jnp.einsum(
            "slqk,sqlc->sklc", dscore, query_part, preferred_element_type=jnp.float32
        )
        dvalue_acc = dvalue_acc + jnp.einsum(
            "slqk,sqlc->sklc",
            prob_full.astype(jnp.bfloat16),
            grad_part,
            preferred_element_type=jnp.float32,
        )
        return (dquery, dkey_acc, dvalue_acc)

    start_state = (
        jnp.zeros(queries.shape, jnp.bfloat16),
        jnp.zeros(key_head_rows.shape, jnp.float32),
        jnp.zeros(value_head_rows.shape, jnp.float32),
    )
    dquery, dkey_acc, dvalue_acc = lax.fori_loop(0, length // block_rows, one_block, start_state)
    return (dquery, dkey_acc.astype(jnp.bfloat16), dvalue_acc.astype(jnp.bfloat16))


def on_device(
    block_in,
    cotangent,
    attention_matrix,
    attention_first_moment,
    attention_second_moment,
    mlp_weight,
    first_mlp,
    second_mlp,
    norm_weight,
    first_norm,
    second_norm,
):
    sequence_count, token_length, feat_width = block_in.shape
    row_count = sequence_count * token_length
    query_total_width = QUERY_HEADS * HEAD_SIZE
    key_value_width = KEY_VALUE_HEADS * HEAD_SIZE
    query_group_count = QUERY_HEADS // KEY_VALUE_HEADS
    whole_attn, gain_rows = (
        lax.all_gather(
            attention_matrix.astype(jnp.bfloat16), ("fsdp", "seq", "mlp"), axis=0, tiled=True
        ),
        lax.all_gather(
            norm_weight.astype(jnp.bfloat16), ("fsdp", "seq", "mlp"), axis=1, tiled=True
        ),
    )
    factor = 1.0 + gain_rows.astype(jnp.float32)
    w_qkv = whole_attn[:, : query_total_width + 2 * key_value_width]
    w_out = whole_attn[:, query_total_width + 2 * key_value_width :]
    tok_rows = block_in.reshape(row_count, feat_width)
    upstream = cotangent.reshape(row_count, feat_width)
    inverse_in = scale_rows(tok_rows)
    normed_in = (tok_rows * inverse_in * factor[0]).astype(jnp.bfloat16)
    query_key_value_rows = jnp.dot(normed_in, w_qkv, preferred_element_type=jnp.float32).astype(
        jnp.bfloat16
    )
    queries = query_key_value_rows[:, :query_total_width].reshape(
        sequence_count, token_length, QUERY_HEADS, HEAD_SIZE
    )
    key_head_rows = jnp.repeat(
        query_key_value_rows[:, query_total_width : query_total_width + key_value_width].reshape(
            sequence_count, token_length, KEY_VALUE_HEADS, HEAD_SIZE
        ),
        query_group_count,
        axis=2,
    )
    value_head_rows = jnp.repeat(
        query_key_value_rows[:, query_total_width + key_value_width :].reshape(
            sequence_count, token_length, KEY_VALUE_HEADS, HEAD_SIZE
        ),
        query_group_count,
        axis=2,
    )
    query_h, key_h, value_h = (
        lax.all_to_all(queries, "seq", split_axis=2, concat_axis=1, tiled=True),
        lax.all_to_all(key_head_rows, "seq", split_axis=2, concat_axis=1, tiled=True),
        lax.all_to_all(value_head_rows, "seq", split_axis=2, concat_axis=1, tiled=True),
    )
    block_rows = min(512, query_h.shape[1])
    mixed_h, totals, saved_state = attend(query_h, key_h, value_h, block_rows)
    mixed = lax.all_to_all(mixed_h, "seq", split_axis=1, concat_axis=2, tiled=True)
    mixed_rows = mixed.reshape(row_count, query_total_width)
    projected = jnp.einsum("rc,dc->rd", mixed_rows, w_out, preferred_element_type=jnp.float32)
    inverse_one = scale_rows(projected)
    middle = tok_rows + projected * inverse_one * factor[1]
    inverse_two = scale_rows(middle)
    normed_mid = (middle * inverse_two * factor[2]).astype(jnp.bfloat16)
    mlp_rows = lax.all_gather(normed_mid, ("seq", "mlp"), axis=0, tiled=True)
    whole_mlp = lax.all_gather(mlp_weight.astype(jnp.bfloat16), "fsdp", axis=1, tiled=True)
    gate_pre = jnp.dot(mlp_rows, whole_mlp[0], preferred_element_type=jnp.float32)
    up_pre = jnp.dot(mlp_rows, whole_mlp[1], preferred_element_type=jnp.float32)
    activated, gelu_back = jax.vjp(gelu_tanh, gate_pre)
    hidden_activation = (activated * up_pre).astype(jnp.bfloat16)
    ffn_part = jnp.einsum(
        "rf,df->rd", hidden_activation, whole_mlp[2], preferred_element_type=jnp.float32
    )
    ffn_out = lax.psum_scatter(
        ffn_part.astype(jnp.bfloat16), ("seq", "mlp"), scatter_dimension=0, tiled=True
    ).astype(jnp.float32)
    inverse_three = scale_rows(ffn_out)
    block_out = middle + ffn_out * inverse_three * factor[3]
    dffn, gain_three = norm_back(ffn_out, inverse_three, factor[3], upstream)
    dffn_rows = lax.all_gather(dffn.astype(jnp.bfloat16), ("seq", "mlp"), axis=0, tiled=True)
    dhidden = jnp.dot(dffn_rows, whole_mlp[2], preferred_element_type=jnp.float32)
    grad_down = jnp.einsum(
        "rd,rf->df", dffn_rows, hidden_activation, preferred_element_type=jnp.float32
    )
    gate_gradient = gelu_back(dhidden * up_pre)[0].astype(jnp.bfloat16)
    up_gradient_half = (dhidden * activated).astype(jnp.bfloat16)
    grad_gate = jnp.einsum("rd,rf->df", mlp_rows, gate_gradient, preferred_element_type=jnp.float32)
    grad_up = jnp.einsum(
        "rd,rf->df", mlp_rows, up_gradient_half, preferred_element_type=jnp.float32
    )
    dnormed_part = jnp.einsum(
        "rf,df->rd", gate_gradient, whole_mlp[0], preferred_element_type=jnp.float32
    ) + jnp.einsum("rf,df->rd", up_gradient_half, whole_mlp[1], preferred_element_type=jnp.float32)
    mlp_grad = lax.psum_scatter(
        jnp.stack([grad_gate, grad_up, grad_down]).astype(jnp.bfloat16),
        "fsdp",
        scatter_dimension=1,
        tiled=True,
    ).astype(jnp.float32)
    dnormed_mid = lax.psum_scatter(
        dnormed_part.astype(jnp.bfloat16), ("seq", "mlp"), scatter_dimension=0, tiled=True
    ).astype(jnp.float32)
    dmid_part, gain_two = norm_back(middle, inverse_two, factor[2], dnormed_mid)
    dmiddle = upstream + dmid_part
    dproj, gain_one = norm_back(projected, inverse_one, factor[1], dmiddle)
    dproj_bf = dproj.astype(jnp.bfloat16)
    dmixed = jnp.dot(dproj_bf, w_out, preferred_element_type=jnp.float32).astype(jnp.bfloat16)
    dmixed_h = lax.all_to_all(
        dmixed.reshape(sequence_count, token_length, QUERY_HEADS, HEAD_SIZE),
        "seq",
        split_axis=2,
        concat_axis=1,
        tiled=True,
    )
    dquery_h, dkey_h, dvalue_h = attend_back(
        query_h, key_h, value_h, mixed_h, totals, dmixed_h, block_rows
    )
    dquery, key_gradient_single, value_gradient_single = (
        lax.all_to_all(dquery_h, "seq", split_axis=1, concat_axis=2, tiled=True),
        lax.all_to_all(dkey_h, "seq", split_axis=1, concat_axis=2, tiled=True),
        lax.all_to_all(dvalue_h, "seq", split_axis=1, concat_axis=2, tiled=True),
    )
    key_gradient = jnp.sum(
        key_gradient_single.astype(jnp.float32).reshape(
            sequence_count, token_length, KEY_VALUE_HEADS, query_group_count, HEAD_SIZE
        ),
        axis=3,
    ).astype(jnp.bfloat16)
    value_gradient = jnp.sum(
        value_gradient_single.astype(jnp.float32).reshape(
            sequence_count, token_length, KEY_VALUE_HEADS, query_group_count, HEAD_SIZE
        ),
        axis=3,
    ).astype(jnp.bfloat16)
    dqkv = jnp.concatenate(
        [
            dquery.reshape(row_count, query_total_width),
            key_gradient.reshape(row_count, key_value_width),
            value_gradient.reshape(row_count, key_value_width),
        ],
        axis=1,
    )
    dnormed_in = jnp.einsum("rc,dc->rd", dqkv, w_qkv, preferred_element_type=jnp.float32)
    dinput_part, gain_zero = norm_back(tok_rows, inverse_in, factor[0], dnormed_in)
    input_grad = dmiddle + dinput_part
    fsdp_count = lax.axis_size("fsdp")
    seq_count = lax.axis_size("seq")
    mlp_count = lax.axis_size("mlp")
    seq_index = lax.axis_index("seq")
    row_share = feat_width // (fsdp_count * seq_count * mlp_count)
    whole_xn, whole_dqkv, whole_dproj, whole_mixed = (
        lax.all_gather(normed_in, "seq", axis=0, tiled=True),
        lax.all_gather(dqkv, "seq", axis=0, tiled=True),
        lax.all_gather(dproj_bf, "seq", axis=0, tiled=True),
        lax.all_gather(mixed_rows, "seq", axis=0, tiled=True),
    )

    def own_columns(values):
        parted = values.reshape(values.shape[0], fsdp_count, seq_count, mlp_count, row_share)
        picked = lax.dynamic_index_in_dim(parted, seq_index, 2, keepdims=False)
        return picked.reshape(values.shape[0], fsdp_count * mlp_count * row_share)

    xn_own = own_columns(whole_xn)
    dproj_own = own_columns(whole_dproj)
    grad_rows = jnp.concatenate(
        [
            jnp.einsum("tr,tc->rc", xn_own, whole_dqkv, preferred_element_type=jnp.float32),
            jnp.einsum("tr,tc->rc", dproj_own, whole_mixed, preferred_element_type=jnp.float32),
        ],
        axis=1,
    )
    attn_grad = lax.psum_scatter(
        grad_rows.astype(jnp.bfloat16), ("fsdp", "mlp"), scatter_dimension=0, tiled=True
    ).astype(jnp.float32)
    norm_grad = lax.psum_scatter(
        jnp.stack([gain_zero, gain_one, gain_two, gain_three]),
        ("fsdp", "seq", "mlp"),
        scatter_dimension=1,
        tiled=True,
    )
    attn_new, first_attn_new, second_attn_new = adam_update(
        attention_matrix, attn_grad, attention_first_moment, attention_second_moment, decay_rate
    )
    mlp_new, first_mlp_new, second_mlp_new = adam_update(
        mlp_weight, mlp_grad, first_mlp, second_mlp, decay_rate
    )
    norm_new, first_norm_new, second_norm_new = adam_update(
        norm_weight, norm_grad, first_norm, second_norm, 0.0
    )
    return (
        block_out.reshape(block_in.shape),
        input_grad.reshape(block_in.shape),
        attn_grad,
        attn_new,
        first_attn_new,
        second_attn_new,
        mlp_grad,
        mlp_new,
        first_mlp_new,
        second_mlp_new,
        norm_grad,
        norm_new,
        first_norm_new,
        second_norm_new,
    )


def solution(mesh):
    placed = (
        P(("fsdp", "mlp"), "seq", None),
        P(("fsdp", "mlp"), "seq", None),
        P(("fsdp", "seq", "mlp"), None),
        P(("fsdp", "seq", "mlp"), None),
        P(("fsdp", "seq", "mlp"), None),
        P(None, "fsdp", ("seq", "mlp")),
        P(None, "fsdp", ("seq", "mlp")),
        P(None, "fsdp", ("seq", "mlp")),
        P(None, ("fsdp", "seq", "mlp")),
        P(None, ("fsdp", "seq", "mlp")),
        P(None, ("fsdp", "seq", "mlp")),
    )
    return jax.shard_map(
        on_device,
        mesh=mesh,
        in_specs=placed,
        out_specs=(
            P(("fsdp", "mlp"), "seq", None),
            P(("fsdp", "mlp"), "seq", None),
            P(("fsdp", "seq", "mlp"), None),
            P(("fsdp", "seq", "mlp"), None),
            P(("fsdp", "seq", "mlp"), None),
            P(("fsdp", "seq", "mlp"), None),
            P(None, "fsdp", ("seq", "mlp")),
            P(None, "fsdp", ("seq", "mlp")),
            P(None, "fsdp", ("seq", "mlp")),
            P(None, "fsdp", ("seq", "mlp")),
            P(None, ("fsdp", "seq", "mlp")),
            P(None, ("fsdp", "seq", "mlp")),
            P(None, ("fsdp", "seq", "mlp")),
            P(None, ("fsdp", "seq", "mlp")),
        ),
        check_vma=False,
    )
```

profile of v0, /device:TPU:0, one launch (start us, length us, event | category | flops | bytes accessed | tf_op | source)
XLA Modules:
  0.0 1472.1 jit_solution(835815689651176044)
XLA Ops:
  8.1 2.5 convert_element_type.191
  10.6 5.6 convert_element_type.194
  16.3 44.5 %all-gather = bf16[32,72,4]{1,2,0:T(4,128)(2,1)S(1)} all-gather(bf16[1,72,4]{1,2,0:T(4,128)(2,1)S(1)} %convert_bitcast_fusion), channel_id=1, replica_groups=mesh['fsdp'=4,'seq'=4,'mlp'=2] {'fsdp','seq','mlp'}, dimensions={0}, use_global_device_ids=true | all-gather | bytes 19008 | tf_op jit(solution)/shard_map/all_gather | solution.py:150
  62.7 121.9 %all-gather.10.cloned.1.call-done = bf16[2304,6144]{1,0:T(8,128)(2,1)} async-done(((bf16[72,6144]{1,0:T(8,128)(2,1)}), bf16[2304,6144]{1,0:T(8,128)(2,1)}) %all-gather.10.cloned.1.call-update) | async-done | bytes 28311568 | tf_op jit(solution)/shard_map/all_gather | solution.py:147
  184.5 9.0 fusion.63
  196.1 3.6 all-to-all-start
  202.7 23.3 %all-to-all-done = bf16[1,256,8,256]{3,1,0,2:T(8,128)(2,1)S(1)} async-done(((bf16[1,256,8,256]{3,1,0,2:T(8,128)(2,1)}), bf16[1,256,8,256]{3,1,0,2:T(8,128)(2,1)S(1)}, u32[]{:S(2)}, u32[]{:S(2)}) %all-to-all-start) | async-done | bytes 1048608 | tf_op jit(solution)/shard_map/all_to_all | solution.py:182
  226.0 2.4 broadcast_in_dim.55
  228.4 4.3 all-to-all-start.1
  234.6 23.7 %all-to-all-done.1 = bf16[1,256,8,256]{3,1,0,2:T(8,128)(2,1)} async-done(((bf16[1,256,8,256]{3,1,0,2:T(8,128)(2,1)}), bf16[1,256,8,256]{3,1,0,2:T(8,128)(2,1)}, u32[]{:S(2)}, u32[]{:S(2)}) %all-to-all-start.1) | async-done | bytes 1048608 | tf_op jit(solution)/shard_map/all_to_all | solution.py:183
  260.4 4.2 all-to-all-start.2
  268.3 21.7 %all-to-all-done.2 = bf16[1,256,8,256]{3,1,0,2:T(8,128)(2,1)} async-done(((bf16[1,256,8,256]{3,1,0,2:T(8,128)(2,1)}), bf16[1,256,8,256]{3,1,0,2:T(8,128)(2,1)}, u32[]{:S(2)}, u32[]{:S(2)}) %all-to-all-start.2) | async-done | bytes 1048608 | tf_op jit(solution)/shard_map/all_to_all | solution.py:184
  293.3 11.7 while.37
  293.7 3.1 select_reduce_fusion.2
  299.6 3.1 select_reduce_fusion.2
  305.0 2.7 copy.91
  307.7 27.9 %all_to_all.120 = bf16[1,1024,2,256]{3,2,0,1:T(2,128)(2,1)S(1)} all-to-all(bf16[1,1024,2,256]{3,2,0,1:T(2,128)(2,1)S(1)} %copy.91), channel_id=1, replica_groups=mesh['fsdp'=4,'seq'=4,'mlp'=2] {'seq'}, dimensions={1} | all-to-all | bytes 2097152 | tf_op jit(solution)/shard_map/all_to_all | solution.py:188
  336.7 2.3 copy.93
  339.0 6.8 multiply_reduce_fusion.5
  350.0 88.9 %all-gather.12.cloned.1.call-done = bf16[2048,2304]{1,0:T(8,128)(2,1)} async-done(((bf16[256,2304]{1,0:T(8,128)(2,1)}), bf16[2048,2304]{1,0:T(8,128)(2,1)}) %all-gather.12.cloned.1.call-update) | async-done | bytes 9437200 | tf_op jit(solution)/shard_map/all_gather | solution.py:195
  439.0 18.1 %fusion.67 = f32[2048,1152]{1,0:T(8,128)} fusion(bf16[2048,2304]{1,0:T(8,128)(2,1)} %all-gather.12.cloned.1.call-done, bf16[3,2304,1152]{2,1,0:T(8,128)(2,1)} %all-gather.14.cloned.1.call-done), kind=kOutput, calls=%fused_computation.98 | convolution fusion | flops 10871635968 | bytes 24182784 | tf_op jit(solution)/shard_map/dot_general | solution.py:197
  457.1 18.7 %multiply_convert_fusion.2 = (bf16[2048,1152]{1,0:T(8,128)(2,1)}, f32[2048,1152]{1,0:T(8,128)}) fusion(f32[2048,1152]{1,0:T(8,128)} %fusion.67, bf16[2048,2304]{1,0:T(8,128)(2,1)S(1)} %copy-done.53, bf16[3,2304,1152]{2,1,0:T(8,128)(2,1)} %all-gather.14.cloned.1.call-done), kind=kOutput, calls=%fused_computation.82 | convolution fusion | flops 10895228928 | bytes 38338560 | tf_op jit(solution)/shard_map/dot_general | solution.py:198
  475.8 18.1 %convolution_convert_fusion.4 = bf16[2048,2304]{1,0:T(8,128)(2,1)} fusion(bf16[2048,1152]{1,0:T(8,128)(2,1)} %get-tuple-element.520, bf16[3,2304,1152]{2,1,0:T(8,128)(2,1)} %all-gather.14.cloned.1.call-done), kind=kOutput, calls=%fused_computation.70 | convolution fusion | flops 10876354560 | bytes 19464192 | tf_op jit(solution)/shard_map/rf,df->rd/dot_general | solution.py:201
  494.2 97.7 %reduce-scatter.6.cloned.1.call-done = bf16[256,2304]{1,0:T(8,128)(2,1)} async-done(((bf16[2048,2304]{1,0:T(8,128)(2,1)}), bf16[256,2304]{1,0:T(8,128)(2,1)}) %reduce-scatter.6.cloned.1.call-update) | async-done | bytes 1179664 | tf_op jit(solution)/shard_map/reduce_scatter | solution.py:204
  593.7 2.6 fusion.88
  597.9 89.3 %all-gather.16.cloned.1.call-done = bf16[2048,2304]{1,0:T(8,128)(2,1)} async-done(((bf16[256,2304]{1,0:T(8,128)(2,1)}), bf16[2048,2304]{1,0:T(8,128)(2,1)}) %all-gather.16.cloned.1.call-update) | async-done | bytes 9437200 | tf_op jit(solution)/shard_map/all_gather | solution.py:210
  687.2 27.8 %multiply_convert_fusion.1 = (bf16[2048,1152]{1,0:T(8,128)(2,1)}, bf16[2048,1152]{1,0:T(8,128)(2,1)}) fusion(f32[2048,1152]{1,0:T(8,128)} %fusion.67, f32[2048,1152]{1,0:T(8,128)} %get-tuple-element.521, bf16[2048,2304]{1,0:T(8,128)(2,1)} %all-gather.16.cloned.1.call-done, bf16[3,2304,1152]{2,1,0:T(8,128)(2,1)} %all-gather.14.cloned.1.call-done), kind=kOutput, calls=%fused_computation.81 | convolution fusion | flops 10928259072 | bytes 43057152 | tf_op jit(solution)/shard_map/dot_general | solution.py:211
  715.0 18.5 %fusion.66 = f32[2048,2304]{1,0:T(8,128)} fusion(bf16[2048,1152]{1,0:T(8,128)(2,1)} %get-tuple-element.514, bf16[3,2304,1152]{2,1,0:T(8,128)(2,1)} %all-gather.14.cloned.1.call-done), kind=kOutput, calls=%fused_computation.97 | convolution fusion | flops 10871635968 | bytes 28901376 | tf_op jit(solution)/shard_map/rf,df->rd/dot_general | solution.py:221
  733.5 21.0 %add_convert_fusion = bf16[2048,2304]{1,0:T(8,128)(2,1)} fusion(f32[2048,2304]{1,0:T(8,128)} %fusion.66, bf16[2048,1152]{1,0:T(8,128)(2,1)} %get-tuple-element.513, bf16[3,2304,1152]{2,1,0:T(8,128)(2,1)} %all-gather.14.cloned.1.call-done), kind=kOutput, calls=%fused_computation.58 | convolution fusion | flops 10881073152 | bytes 38338560 | tf_op jit(solution)/shard_map/rf,df->rd/dot_general | solution.py:223
  755.1 173.4 %reduce-scatter.8.cloned.1.call-done = bf16[256,2304]{1,0:T(8,128)(2,1)} async-done(((bf16[2048,2304]{1,0:T(8,128)(2,1)}), bf16[256,2304]{1,0:T(8,128)(2,1)}) %reduce-scatter.8.cloned.1.call-update) | async-done | bytes 1179664 | tf_op jit(solution)/shard_map/reduce_scatter | solution.py:230
  928.6 2.9 fusion.90
  931.5 4.9 multiply_reduce_fusion
  939.4 6.7 fusion.76
  947.6 4.4 all-to-all-start.4
  952.5 52.4 %all-to-all-done.4 = bf16[1,256,8,256]{3,1,0,2:T(8,128)(2,1)} async-done(((bf16[1,256,8,256]{3,1,0,2:T(8,128)(2,1)}), bf16[1,256,8,256]{3,1,0,2:T(8,128)(2,1)}, u32[]{:S(2)}, u32[]{:S(2)}) %all-to-all-start.4) | async-done | bytes 1048608 | tf_op jit(solution)/shard_map/all_to_all | solution.py:238
  1010.3 22.0 %while.38 = (s32[]{:T(128)}, bf16[1,1024,2,256]{3,2,0,1:T(2,128)(2,1)}, f32[1,1024,2,256]{1,3,2,0:T(8,128)S(1)}, f32[1,1024,2,256]{1,3,2,0:T(8,128)}, bf16[1,102...) while((s32[]{:T(128)}, ...), condition=%wide.region_14.15_spmd.clone, body=%wide.region_13.14_spmd.clone.sunk | while | flops 2704015872 | bytes 73433512 | solution.py:124
  1013.1 2.6 multiply_convert_fusion.7
  1024.1 2.6 multiply_convert_fusion.7
  1032.4 2.9 copy.103
  1035.3 36.2 %all_to_all.121 = bf16[1,1024,2,256]{3,2,0,1:T(2,128)(2,1)} all-to-all(bf16[1,1024,2,256]{3,2,0,1:T(2,128)(2,1)S(1)} %copy.103), channel_id=1, replica_groups=mesh['fsdp'=4,'seq'=4,'mlp'=2] {'seq'}, dimensions={1} | all-to-all | bytes 2097152 | tf_op jit(solution)/shard_map/all_to_all | solution.py:251
  1071.5 3.5 all-to-all-start.5
  1077.3 56.2 %all-to-all-done.5 = bf16[1,1024,2,256]{3,2,0,1:T(2,128)(2,1)S(1)} async-done(((bf16[1,1024,2,256]{3,2,0,1:T(2,128)(2,1)}), bf16[1,1024,2,256]{3,2,0,1:T(2,128)(2,1)S(1)}, u32[]{:S(2)}, u32[]{:S(2)}) %all-to-all-start.5) | async-done | bytes 1048608 | tf_op jit(solution)/shard_map/all_to_all | solution.py:249
  1133.5 3.5 all-to-all-start.6
  1137.1 3.8 reduce_sum.164
  1142.8 41.8 %all-to-all-done.6 = bf16[1,1024,2,256]{3,2,0,1:T(2,128)(2,1)S(1)} async-done(((bf16[1,1024,2,256]{3,2,0,1:T(2,128)(2,1)}), bf16[1,1024,2,256]{3,2,0,1:T(2,128)(2,1)S(1)}, u32[]{:S(2)}, u32[]{:S(2)}) %all-to-all-start.6) | async-done | bytes 1048608 | tf_op jit(solution)/shard_map/all_to_all | solution.py:250
  1184.7 2.7 reduce_sum.163
  1187.6 2.7 pad_maximum_fusion.2
  1190.5 16.4 %fusion.50 = bf16[1,2304,1152]{2,1,0:T(8,128)(2,1)S(1)} fusion(bf16[2048,2304]{1,0:T(8,128)(2,1)} %all-gather.16.cloned.1.call-done, bf16[2048,1152]{1,0:T(8,128)(2,1)} %get-tuple-element.520), kind=kOutput, calls=%fused_computation.73 | convolution fusion | flops 10874290176 | bytes 19464192 | tf_op jit(solution)/shard_map/rd,rf->df/dot_general | solution.py:212
  1206.9 16.5 %fusion.49 = bf16[1,2304,1152]{2,1,0:T(8,128)(2,1)S(1)} fusion(bf16[2048,2304]{1,0:T(8,128)(2,1)} %all-gather.12.cloned.1.call-done, bf16[2048,1152]{1,0:T(8,128)(2,1)} %get-tuple-element.513), kind=kOutput, calls=%fused_computation.72 | convolution fusion | flops 10874290176 | bytes 19464192 | tf_op jit(solution)/shard_map/rd,rf->df/dot_general | solution.py:218
  1223.5 13.4 fusion.48
  1236.9 7.0 pad_maximum_fusion
  1244.0 7.0 copy.107
  1251.0 2.4 constant_dynamic-slice_fusion.2
  1253.4 6.7 copy.108
  1261.6 6.3 convolution_convert_fusion.6
  1267.9 71.6 %all-gather.20.cloned.1.call-done = bf16[1024,4096]{0,1:T(8,128)(2,1)} async-done(((bf16[256,4096]{0,1:T(8,128)(2,1)}), bf16[1024,4096]{0,1:T(8,128)(2,1)}) %all-gather.20.cloned.1.call-update) | async-done | bytes 8388624 | tf_op jit(solution)/shard_map/all_gather | solution.py:283
  1339.5 7.8 convolution_convert_fusion.5
  1347.3 5.4 pad_maximum_fusion.1
  1355.0 11.5 multiply_reduce_fusion.1
  1366.5 40.1 %all-reduce = f32[4,2304]{1,0:T(4,128)S(1)} all-reduce(f32[4,2304]{1,0:T(4,128)S(1)} %pad_maximum_fusion.3), channel_id=6, replica_groups=mesh['fsdp'=4,'seq'=4,'mlp'=2] {'fsdp','seq','mlp'}, use_global_device_ids=true, to_apply=%region_24.25.clone | all-reduce | flops 9216 | bytes 73728
  1407.3 4.7 add_bitcast_fusion
  1412.0 21.8 %multiply_subtract_fusion = (f32[3,576,1152]{2,1,0:T(8,128)}, f32[3,576,1152]{2,1,0:T(8,128)}, f32[3,576,1152]{2,1,0:T(8,128)}, f32[3,576,1152]{2,1,0:T(8,128)}) fusion(f32[3,576,1152]{2,1,0:T(8,128)} %param.20, f32[3,576,1152]{2,1,0:T(8,128)} %param.21, f32[3,576,1152]{2,1,0:T(8,128)} %param.22, bf16[3,576,1152]{2,1,0:T(8,128)(2,1)} %reduce-scatter.12.cloned.1.call-done), kind=kLoop, calls=%fused_computation.89 | loop fusion | flops 31850496 | bytes 59719680 | tf_op jit(solution)/shard_map/sub | solution.py:41
  1433.8 25.4 %reduce-scatter.10.cloned.1.call-done = bf16[72,6144]{1,0:T(8,128)(2,1)} async-done(((bf16[576,6144]{1,0:T(8,128)(2,1)}), bf16[72,6144]{1,0:T(8,128)(2,1)}) %reduce-scatter.10.cloned.1.call-update) | async-done | bytes 884752 | tf_op jit(solution)/shard_map/reduce_scatter | solution.py:302
  1459.2 5.1 multiply_subtract_fusion.1
  (248 shorter events, 69.1 us)
Async XLA Ops:
  8.0 176.5 %all-gather.10.cloned.1.call-start = ((), (), s32[]{:S(2)}) async-start(), calls=%async_computation.12 | async-start | bytes 29196288 | tf_op jit(solution)/shard_map/all_gather | solution.py:147
  10.6 5.7 copy-start.49
  10.6 339.4 %all-gather.14.cloned.1.call-start = ((), (), s32[]{:S(2)}) async-start(), calls=%async_computation.14 | async-start | bytes 19906560 | tf_op jit(solution)/shard_map/all_gather | solution.py:196
  16.2 45.3 %copy-start.4 = (f32[1,256,2304]{2,1,0:T(8,128)S(1)}, f32[1,256,2304]{2,1,0:T(8,128)}, u32[]{:S(2)}) copy-start(f32[1,256,2304]{2,1,0:T(8,128)} %param.15) | copy-start | bytes 7077892
  61.6 284.3 %copy-start.32 = (f32[2304]{0:T(1024)}, f32[2304]{0:T(1024)S(1)}, u32[]{:S(2)}) copy-start(f32[2304]{0:T(1024)S(1)} %get-tuple-element.462) | copy-start | bytes 27652
  62.7 130.9 %copy-start.17 = (bf16[256,2304]{1,0:T(8,128)(2,1)}, bf16[256,2304]{1,0:T(8,128)(2,1)S(1)}, u32[]{:S(2)}) copy-start(bf16[256,2304]{1,0:T(8,128)(2,1)S(1)} %multiply_convert_fusion.5) | copy-start | bytes 3538948
  196.1 29.9 %all-to-all-start = ((bf16[1,256,8,256]{3,1,0,2:T(8,128)(2,1)}), bf16[1,256,8,256]{3,1,0,2:T(8,128)(2,1)S(1)}, u32[]{:S(2)}, u32[]{:S(2)}) async-start(bf16[1,256,8,256]{3,1,0,2:T(8,128)(2,1)} %copy.85), calls=%async_computation | async-start | bytes 2097152 | tf_op jit(solution)/shard_map/all_to_all | solution.py:182
  226.0 34.4 %copy-start.20 = (bf16[1,256,8,256]{3,1,0,2:T(8,128)(2,1)}, bf16[1,256,8,256]{3,1,0,2:T(8,128)(2,1)S(1)}, u32[]{:S(2)}) copy-start(bf16[1,256,8,256]{3,1,0,2:T(8,128)(2,1)S(1)} %all-to-all-done) | copy-start | bytes 3145732
  228.4 29.9 %all-to-all-start.1 = ((bf16[1,256,8,256]{3,1,0,2:T(8,128)(2,1)}), bf16[1,256,8,256]{3,1,0,2:T(8,128)(2,1)}, u32[]{:S(2)}, u32[]{:S(2)}) async-start(bf16[1,256,8,256]{3,1,0,2:T(8,128)(2,1)} %bitcast.242), calls=%async_computation.1 | async-start | bytes 2097152 | tf_op jit(solution)/shard_map/all_to_all | solution.py:183
  260.4 29.6 %all-to-all-start.2 = ((bf16[1,256,8,256]{3,1,0,2:T(8,128)(2,1)}), bf16[1,256,8,256]{3,1,0,2:T(8,128)(2,1)}, u32[]{:S(2)}, u32[]{:S(2)}) async-start(bf16[1,256,8,256]{3,1,0,2:T(8,128)(2,1)} %bitcast.241), calls=%async_computation.2 | async-start | bytes 2097152 | tf_op jit(solution)/shard_map/all_to_all | solution.py:184
  264.6 174.3 %all-gather.12.cloned.1.call-start = ((), (), s32[]{:S(2)}) async-start(), calls=%async_computation.13 | async-start | bytes 10616832 | tf_op jit(solution)/shard_map/all_gather | solution.py:195
  293.7 3.2 copy-start.13
  293.7 3.2 copy-start.30
  299.5 3.2 copy-start.13
  299.6 3.2 copy-start.30
  305.0 34.0 %copy-start = (bf16[1,1024,2,256]{3,1,2,0:T(8,128)(2,1)}, bf16[1,1024,2,256]{3,1,2,0:T(8,128)(2,1)S(1)}, u32[]{:S(2)}) copy-start(bf16[1,1024,2,256]{3,1,2,0:T(8,128)(2,1)S(1)} %get-tuple-element.711) | copy-start | bytes 3145732
  305.0 34.0 %copy-start.38 = (f32[1,2,1024]{2,1,0:T(2,128)}, f32[1,2,1024]{2,1,0:T(2,128)S(1)}, u32[]{:S(2)}) copy-start(f32[1,2,1024]{2,1,0:T(2,128)S(1)} %get-tuple-element.661) | copy-start | bytes 24580
  345.8 2.8 copy-start.35
  345.8 4.1 copy-start.43
  349.9 242.0 %reduce-scatter.6.cloned.1.call-start = ((), (), s32[]{:S(2)}) async-start(), calls=%async_computation.15 | async-start | bytes 10616832 | tf_op jit(solution)/shard_map/reduce_scatter | solution.py:204
  439.0 18.1 %copy-start.53 = (bf16[2048,2304]{1,0:T(8,128)(2,1)S(1)}, bf16[2048,2304]{1,0:T(8,128)(2,1)}, u32[]{:S(2)}) copy-start(bf16[2048,2304]{1,0:T(8,128)(2,1)} %all-gather.12.cloned.1.call-done) | copy-start | bytes 28311556
  493.9 99.7 %copy-start.7 = (f32[1,256,2304]{2,1,0:T(8,128)S(1)}, f32[1,256,2304]{2,1,0:T(8,128)}, u32[]{:S(2)}) copy-start(f32[1,256,2304]{2,1,0:T(8,128)} %param.16) | copy-start | bytes 7077892
  493.9 99.7 %copy-start.34 = (f32[2304]{0:T(1024)S(1)}, f32[2304]{0:T(1024)}, u32[]{:S(2)}) copy-start(f32[2304]{0:T(1024)} %get-tuple-element.460) | copy-start | bytes 27652
  494.0 193.2 %all-gather.16.cloned.1.call-start = ((), (), s32[]{:S(2)}) async-start(), calls=%async_computation.16 | async-start | bytes 10616832 | tf_op jit(solution)/shard_map/all_gather | solution.py:210
  592.0 4.3 copy-start.12
  593.6 2.6 copy-start.46
  597.9 330.7 %reduce-scatter.8.cloned.1.call-start = ((), (), s32[]{:S(2)}) async-start(), calls=%async_computation.17 | async-start | bytes 10616832 | tf_op jit(solution)/shard_map/reduce_scatter | solution.py:230
  754.5 174.1 %copy-start.3 = (f32[256,2304]{1,0:T(8,128)S(1)}, f32[256,2304]{1,0:T(8,128)}, u32[]{:S(2)}) copy-start(f32[256,2304]{1,0:T(8,128)} %copy-done.2) | copy-start | bytes 7077892
  754.5 177.0 %copy-start.33 = (f32[2304]{0:T(1024)S(1)}, f32[2304]{0:T(1024)}, u32[]{:S(2)}) copy-start(f32[2304]{0:T(1024)} %copy-done.32) | copy-start | bytes 27652
  754.5 177.0 %copy-start.44 = (f32[256]{0:T(256)S(1)}, f32[256]{0:T(256)}, u32[]{:S(2)}) copy-start(f32[256]{0:T(256)} %copy-done.43) | copy-start | bytes 3076
  754.5 489.5 %all-gather.18.cloned.1.call-start = ((), (), s32[]{:S(2)}) async-start(), calls=%async_computation.18 | async-start | bytes 5898240 | tf_op jit(solution)/shard_map/all_gather | solution.py:282
  755.1 498.3 %all-gather.22.cloned.1.call-start = ((), (), s32[]{:S(2)}) async-start(), calls=%async_computation.20 | async-start | bytes 5898240 | tf_op jit(solution)/shard_map/all_gather | solution.py:284
  928.6 2.9 copy-start.8
  928.6 2.9 copy-start.16
  931.5 6.3 copy-start.11
  947.5 62.8 %copy-start.1 = (bf16[1,1024,2,256]{3,1,2,0:T(8,128)(2,1)S(1)}, bf16[1,1024,2,256]{3,1,2,0:T(8,128)(2,1)}, u32[]{:S(2)}) copy-start(bf16[1,1024,2,256]{3,1,2,0:T(8,128)(2,1)} %copy-done) | copy-start | bytes 3145732
  947.6 62.8 %copy-start.39 = (f32[1,2,1024]{2,1,0:T(2,128)S(1)}, f32[1,2,1024]{2,1,0:T(2,128)}, u32[]{:S(2)}) copy-start(f32[1,2,1024]{2,1,0:T(2,128)} %copy-done.38) | copy-start | bytes 24580
  947.6 57.4 %all-to-all-start.4 = ((bf16[1,256,8,256]{3,1,0,2:T(8,128)(2,1)}), bf16[1,256,8,256]{3,1,0,2:T(8,128)(2,1)}, u32[]{:S(2)}, u32[]{:S(2)}) async-start(bf16[1,256,8,256]{3,1,0,2:T(8,128)(2,1)} %copy.94), calls=%async_computation.6 | async-start | bytes 2097152 | tf_op jit(solution)/shard_map/all_to_all | solution.py:238
  951.9 309.6 %all-gather.24.cloned.1.call-start = ((), (), s32[]{:S(2)}) async-start(), calls=%async_computation.21 | async-start | bytes 5242880 | tf_op jit(solution)/shard_map/all_gather | solution.py:285
  1010.5 2.6 copy-start.19
  1010.5 2.6 copy-start.31
  1013.1 2.6 copy-start.25
  1021.5 2.6 copy-start.19
  1021.5 2.6 copy-start.31
  1024.1 2.6 copy-start.25
  1071.5 62.0 %all-to-all-start.5 = ((bf16[1,1024,2,256]{3,2,0,1:T(2,128)(2,1)}), bf16[1,1024,2,256]{3,2,0,1:T(2,128)(2,1)S(1)}, u32[]{:S(2)}, u32[]{:S(2)}) async-start(bf16[1,1024,2,256]{3,2,0,1:T(2,128)(2,1)} %get-tuple-element.416), calls=%async_computation.7 | async-start | bytes 2097152 | tf_op jit(solution)/shard_map/all_to_all | solution.py:249
  1133.5 51.1 %all-to-all-start.6 = ((bf16[1,1024,2,256]{3,2,0,1:T(2,128)(2,1)}), bf16[1,1024,2,256]{3,2,0,1:T(2,128)(2,1)S(1)}, u32[]{:S(2)}, u32[]{:S(2)}) async-start(bf16[1,1024,2,256]{3,2,0,1:T(2,128)(2,1)} %copy.99), calls=%async_computation.8 | async-start | bytes 2097152 | tf_op jit(solution)/shard_map/all_to_all | solution.py:250
  1137.1 202.4 %all-gather.20.cloned.1.call-start = ((), (), s32[]{:S(2)}) async-start(), calls=%async_computation.19 | async-start | bytes 10485760 | tf_op jit(solution)/shard_map/all_gather | solution.py:283
  1142.8 47.6 %copy-start.23 = (bf16[1,256,4,2,256]{1,4,3,2,0:T(8,128)(2,1)}, bf16[1,256,4,2,256]{1,4,3,2,0:T(8,128)(2,1)S(1)}, u32[]{:S(2)}) copy-start(bf16[1,256,4,2,256]{1,4,3,2,0:T(8,128)(2,1)S(1)} %copy.98) | copy-start | bytes 3145732
  1187.6 19.3 %copy-start.28 = (bf16[256,4,256]{0,2,1:T(8,128)(2,1)}, bf16[256,4,256]{0,2,1:T(8,128)(2,1)S(1)}, u32[]{:S(2)}) copy-start(bf16[256,4,256]{0,2,1:T(8,128)(2,1)S(1)} %copy.102) | copy-start | bytes 1572868
  1190.4 221.6 %reduce-scatter.12.cloned.1.call-start = ((), (), s32[]{:S(2)}) async-start(), calls=%async_computation.23 | async-start | bytes 19906560 | tf_op jit(solution)/shard_map/reduce_scatter | solution.py:224
  1190.4 33.0 %slice-start = ((s8[9437184]{0:T(1024)(128)(4,1)}), s8[4194304]{0:T(1024)(128)(4,1)S(1)}, s32[]{:S(2)}) async-start(s8[9437184]{0:T(1024)(128)(4,1)} %bitcast.266), calls=%async_computation.24 | async-start | bytes 8388608
  1190.4 33.0 %slice-start.1 = ((s8[9437184]{0:T(1024)(128)(4,1)}), s8[4194304]{0:T(1024)(128)(4,1)S(1)}, s32[]{:S(2)}) async-start(s8[9437184]{0:T(1024)(128)(4,1)} %bitcast.266), calls=%async_computation.25 | async-start | bytes 8388608
  1190.4 33.0 %slice-start.3 = ((s8[4718592]{0:T(1024)(128)(4,1)}), s8[4194304]{0:T(1024)(128)(4,1)S(1)}, s32[]{:S(2)}) async-start(s8[4718592]{0:T(1024)(128)(4,1)} %bitcast.268), calls=%async_computation.27 | async-start | bytes 8388608
  1206.9 16.6 %slice-start.2 = ((s8[9437184]{0:T(1024)(128)(4,1)}), s8[1048576]{0:T(1024)(128)(4,1)S(1)}, s32[]{:S(2)}) async-start(s8[9437184]{0:T(1024)(128)(4,1)} %bitcast.266), calls=%async_computation.26 | async-start | bytes 2097152
  1206.9 16.6 %slice-start.4 = ((s8[4718592]{0:T(1024)(128)(4,1)}), s8[524288]{0:T(1024)(128)(4,1)S(1)}, s32[]{:S(2)}) async-start(s8[4718592]{0:T(1024)(128)(4,1)} %bitcast.268), calls=%async_computation.28 | async-start | bytes 1048576
  1243.9 215.2 %reduce-scatter.10.cloned.1.call-start = ((), (), s32[]{:S(2)}) async-start(), calls=%async_computation.22 | async-start | bytes 7962624 | tf_op jit(solution)/shard_map/reduce_scatter | solution.py:302
  1352.7 2.3 copy-start.24
  1352.7 2.3 copy-start.37
  1355.0 51.6 %copy-start.50 = (f32[4,72]{1,0:T(4,128)S(1)}, f32[4,72]{1,0:T(4,128)}, u32[]{:S(2)}) copy-start(f32[4,72]{1,0:T(4,128)} %param.23) | copy-start | bytes 3460
  1355.0 51.6 %copy-start.51 = (f32[4,72]{1,0:T(4,128)S(1)}, f32[4,72]{1,0:T(4,128)}, u32[]{:S(2)}) copy-start(f32[4,72]{1,0:T(4,128)} %param.24) | copy-start | bytes 3460
  1355.0 51.6 %copy-start.52 = (f32[4,72]{1,0:T(4,128)S(1)}, f32[4,72]{1,0:T(4,128)}, u32[]{:S(2)}) copy-start(f32[4,72]{1,0:T(4,128)} %param.25) | copy-start | bytes 3460
  1412.0 47.1 %copy-start.15 = (f32[72,6144]{1,0:T(8,128)S(1)}, f32[72,6144]{1,0:T(8,128)}, u32[]{:S(2)}) copy-start(f32[72,6144]{1,0:T(8,128)} %param.17) | copy-start | bytes 5308420
  1412.0 47.1 %copy-start.29 = (f32[72,6144]{1,0:T(8,128)S(1)}, f32[72,6144]{1,0:T(8,128)}, u32[]{:S(2)}) copy-start(f32[72,6144]{1,0:T(8,128)} %param.18) | copy-start | bytes 5308420
  (23 other events, 29.7 us)
Sparse Core Ops, SparseCore 0:
  12.4 172.0 all-gather.9
  186.9 148.3 all-gather.13
  350.1 88.8 all-gather.11
  494.1 97.8 reduce-scatter.5
  598.0 89.1 all-gather.15
  754.6 173.9 reduce-scatter.7
  1244.0 145.9 reduce-scatter.11
  1393.6 65.4 reduce-scatter.9
Sparse Core Ops, SparseCore 1:
  757.1 131.4 all-gather.17
  939.5 128.1 all-gather.21
  1069.1 120.7 all-gather.23
  1191.5 147.9 all-gather.19
where the time goes:
time: 1480 us; the launch traced here: 1470 us
  waiting for transfers between devices  889 us (60%)
  matrix products  243 us (16%)
  blocking collectives  149 us (10%)
  other arithmetic  82.7 us (6%)
  local copies, waits for them, and re-layouts  67.6 us (5%)
  starting transfers between devices  24.2 us (2%)
  between operations  16.7 us (1%)
    reduce_scatter x1, waiting for transfers between devices, on_device(): lax.psum_scatter(dnormed_part.astype(jnp.bfloat16), ('seq', 'mlp'), scatt...  173 us
    all_gather x1, waiting for transfers between devices, on_device(): lax.all_gather(attention_matrix.astype(jnp.bfloat16), ('fsdp', 'seq', 'ml...  122 us
    reduce_scatter x1, waiting for transfers between devices, on_device(): lax.psum_scatter(ffn_part.astype(jnp.bfloat16), ('seq', 'mlp'), scatter_d...  97.7 us
    all_gather x1, waiting for transfers between devices, on_device(): lax.all_gather(dffn.astype(jnp.bfloat16), ('seq', 'mlp'), axis=0, tiled=T...  89.3 us
    all_gather x1, waiting for transfers between devices, on_device(): mlp_rows = lax.all_gather(normed_mid, ('seq', 'mlp'), axis=0, tiled=True)  88.9 us
    all_gather x1, waiting for transfers between devices, on_device(): lax.all_gather(dqkv, 'seq', axis=0, tiled=True)  71.6 us
    all_to_all x1, waiting for transfers between devices, on_device(): lax.all_to_all(dquery_h, 'seq', split_axis=1, concat_axis=2, tiled=True)  56.2 us
    all_to_all x1, waiting for transfers between devices, on_device(): lax.all_to_all(dmixed.reshape(sequence_count, token_length, QUERY_HEADS,...  52.4 us
  transfers between devices with their start and end apart: 18, of which 13 were waited for; matrix products, arithmetic and copies ran while one was open for 17% of the time, Pallas kernels for 0%

commit v1 on v0

--- a/solution.py
+++ b/solution.py
@@ -1,6 +1,11 @@
+import functools
+import math
+
 import jax
 import jax.numpy as jnp
 from jax import lax
+from jax.experimental import pallas as pl
+from jax.experimental.pallas import tpu as pltpu
 from jax.sharding import PartitionSpec as P
 
 QUERY_HEADS = 8
@@ -16,6 +21,9 @@
 learn_rate = 0.01
 decay_rate = 0.1
 step_count = 2
+gelu_scale = math.sqrt(2.0 / math.pi)
+gelu_cubic = 0.044715
+mlp_chunks = 4
 
 
 def scale_rows(values):
@@ -125,7 +133,7 @@
     return (dquery, dkey_acc.astype(jnp.bfloat16), dvalue_acc.astype(jnp.bfloat16))
 
 
-def on_device(
+def on_device_generic(
     block_in,
     cotangent,
     attention_matrix,
@@ -335,7 +343,814 @@
     )
 
 
+MESH = pl.DeviceIdType.MESH
+AXES = ("fsdp", "seq", "mlp")
+
+
+def exchange_kernel(sizes, mine_ref, out_ref, send_sem, recv_sem):
+    n_fsdp, n_seq, n_mlp = sizes
+    count = n_fsdp * n_seq * n_mlp
+    me = (lax.axis_index("fsdp") * n_seq + lax.axis_index("seq")) * n_mlp + lax.axis_index("mlp")
+    slots = mine_ref.shape[0]
+
+    def place(index):
+        return (index // (n_seq * n_mlp), (index // n_mlp) % n_seq, index % n_mlp)
+
+    barrier = pltpu.get_barrier_semaphore()
+
+    @pl.loop(1, count)
+    def _(step):
+        pl.semaphore_signal(barrier, inc=1, device_id=place((me + step) % count), device_id_type=MESH)
+
+    pl.semaphore_wait(barrier, count - 1)
+
+    def copy_to(step):
+        to = (me + step) % count
+        return pltpu.make_async_remote_copy(
+            src_ref=mine_ref.at[to % slots],
+            dst_ref=out_ref.at[me],
+            send_sem=send_sem.at[step],
+            recv_sem=recv_sem.at[step],
+            device_id=place(to),
+            device_id_type=MESH,
+        )
+
+    @pl.loop(1, count)
+    def _(step):
+        copy_to(step).start()
+
+    out_ref[pl.ds(me, 1)] = mine_ref[pl.ds(me % slots, 1)]
+
+    @pl.loop(1, count)
+    def _(step):
+        copy_to(step).wait()
+
+
+def exchange(sizes, mine, collective_id):
+    count = sizes[0] * sizes[1] * sizes[2]
+    return pl.pallas_call(
+        functools.partial(exchange_kernel, sizes),
+        out_shape=jax.ShapeDtypeStruct((count,) + mine.shape[1:], mine.dtype),
+        in_specs=[pl.BlockSpec(memory_space=pltpu.VMEM)],
+        out_specs=pl.BlockSpec(memory_space=pltpu.VMEM),
+        scratch_shapes=[pltpu.SemaphoreType.DMA((count,)), pltpu.SemaphoreType.DMA((count,))],
+        compiler_params=pltpu.CompilerParams(collective_id=collective_id, has_side_effects=True),
+    )(mine)
+
+
+def neighbour_barrier(seq_count, at, up, down, sibling):
+    barrier = pltpu.get_barrier_semaphore()
+
+    @pl.when(at < seq_count - 1)
+    def _():
+        pl.semaphore_signal(barrier, inc=1, device_id=up, device_id_type=MESH)
+
+    @pl.when(at > 0)
+    def _():
+        pl.semaphore_signal(barrier, inc=1, device_id=down, device_id_type=MESH)
+
+    peers = jnp.where(at < seq_count - 1, 1, 0) + jnp.where(at > 0, 1, 0)
+    if sibling is not None:
+        pl.semaphore_signal(barrier, inc=1, device_id=sibling, device_id_type=MESH)
+        peers = peers + 1
+    pl.semaphore_wait(barrier, peers)
+
+
+class RowGather:
+    def __init__(self, n, own, whole, send_sem, recv_sem):
+        self.n, self.own, self.whole = n, own, whole
+        self.send_sem, self.recv_sem = send_sem, recv_sem
+        self.fsdp, self.at, self.core = (
+            lax.axis_index("fsdp"),
+            lax.axis_index("seq"),
+            lax.axis_index("mlp"),
+        )
+        self.up = (self.fsdp, lax.rem(self.at + 1, n), self.core)
+        self.down = (self.fsdp, lax.rem(self.at + n - 1, n), self.core)
+        self.sibling = (self.fsdp, self.at, 1 - self.core)
+
+    def copy(self, chunk, block, way, own=False):
+        slot = self.core * self.n + block
+        return pltpu.make_async_remote_copy(
+            src_ref=self.own.at[chunk] if own else self.whole.at[chunk, slot],
+            dst_ref=self.whole.at[chunk, slot],
+            send_sem=self.send_sem.at[chunk, way, block],
+            recv_sem=self.recv_sem.at[chunk, slot],
+            device_id=(self.up, self.down, self.sibling)[way],
+            device_id_type=MESH,
+        )
+
+    def arrival(self, chunk, slot):
+        return pltpu.make_async_remote_copy(
+            src_ref=self.own.at[chunk],
+            dst_ref=self.whole.at[chunk, slot],
+            send_sem=self.send_sem.at[chunk, 0, 0],
+            recv_sem=self.recv_sem.at[chunk, slot],
+            device_id=self.sibling,
+            device_id_type=MESH,
+        )
+
+    def begin(self, chunk):
+        @pl.when(self.at < self.n - 1)
+        def _():
+            self.copy(chunk, self.at, 0, True).start()
+
+        @pl.when(self.at > 0)
+        def _():
+            self.copy(chunk, self.at, 1, True).start()
+
+        self.copy(chunk, self.at, 2, True).start()
+
+    def step(self, chunk, hop):
+        below, above = self.at - hop, self.at + hop
+
+        @pl.when(below >= 0)
+        def _():
+            self.arrival(chunk, self.core * self.n + below).wait_recv()
+
+            @pl.when(self.at < self.n - 1)
+            def _():
+                self.copy(chunk, below, 0).start()
+
+            self.copy(chunk, below, 2).start()
+
+        @pl.when(above < self.n)
+        def _():
+            self.arrival(chunk, self.core * self.n + above).wait_recv()
+
+            @pl.when(self.at > 0)
+            def _():
+                self.copy(chunk, above, 1).start()
+
+            self.copy(chunk, above, 2).start()
+
+    def finish(self, chunk):
+        for block in range(self.n):
+            self.arrival(chunk, (1 - self.core) * self.n + block).wait_recv()
+
+    def drain(self, chunk):
+        for block in range(self.n):
+
+            @pl.when((block <= self.at) & (self.at < self.n - 1))
+            def _():
+                self.copy(chunk, block, 0).wait_send()
+
+            @pl.when((block >= self.at) & (self.at > 0))
+            def _():
+                self.copy(chunk, block, 1).wait_send()
+
+            self.copy(chunk, block, 2).wait_send()
+
+
+class RowScatter:
+    def __init__(self, n, total, held, send_sem, recv_sem):
+        self.n, self.total, self.held = n, total, held
+        self.send_sem, self.recv_sem = send_sem, recv_sem
+        self.fsdp, self.at, self.core = (
+            lax.axis_index("fsdp"),
+            lax.axis_index("seq"),
+            lax.axis_index("mlp"),
+        )
+        self.up = (self.fsdp, lax.rem(self.at + 1, n), self.core)
+        self.down = (self.fsdp, lax.rem(self.at + n - 1, n), self.core)
+
+    def copy(self, chunk, block, way):
+        slot = block
+        if way == 1:
+            slot = jnp.where(block == self.at - 1, self.n, block)
+        return pltpu.make_async_remote_copy(
+            src_ref=self.total.at[chunk, block],
+            dst_ref=self.held.at[chunk, slot],
+            send_sem=self.send_sem.at[chunk, way, block],
+            recv_sem=self.recv_sem.at[chunk, slot],
+            device_id=(self.up, self.down)[way],
+            device_id_type=MESH,
+        )
+
+    def arrive(self, chunk, slot):
+        pltpu.make_async_remote_copy(
+            src_ref=self.total.at[chunk, 0],
+            dst_ref=self.held.at[chunk, slot],
+            send_sem=self.send_sem.at[chunk, 0, 0],
+            recv_sem=self.recv_sem.at[chunk, slot],
+            device_id=self.up,
+            device_id_type=MESH,
+        ).wait_recv()
+
+    def add(self, chunk, block):
+        self.arrive(chunk, block)
+        self.total[chunk, block] = (
+            self.total[chunk, block].astype(jnp.float32)
+            + self.held[chunk, block].astype(jnp.float32)
+        ).astype(jnp.bfloat16)
+
+    def step(self, chunk, wave):
+        far = self.n - 1 - self.at
+
+        @pl.when(self.at < wave)
+        def _():
+            block = self.n - wave + self.at
+
+            @pl.when(self.at > 0)
+            def _():
+                self.add(chunk, block)
+
+            self.copy(chunk, block, 0).start()
+
+        @pl.when(far < wave)
+        def _():
+            block = wave - 1 - far
+
+            @pl.when(far > 0)
+            def _():
+                self.add(chunk, block)
+
+            self.copy(chunk, block, 1).start()
+
+    def finish(self, chunk, store):
+        own = self.total[chunk, self.at].astype(jnp.float32)
+        last = self.n - 1
+
+        @pl.when(self.at == 0)
+        def _():
+            self.arrive(chunk, self.n)
+            store(own + self.held[chunk, self.n].astype(jnp.float32))
+
+        @pl.when(self.at == last)
+        def _():
+            self.arrive(chunk, self.at)
+            store(own + self.held[chunk, self.at].astype(jnp.float32))
+
+        @pl.when((self.at > 0) & (self.at < last))
+        def _():
+            self.arrive(chunk, self.at)
+            self.arrive(chunk, self.n)
+            store(
+                own
+                + self.held[chunk, self.at].astype(jnp.float32)
+                + self.held[chunk, self.n].astype(jnp.float32)
+            )
+
+    def drain(self, chunk):
+        for block in range(self.n):
+
+            @pl.when(block > self.at)
+            def _():
+                self.copy(chunk, block, 0).wait_send()
+
+            @pl.when(block < self.at)
+            def _():
+                self.copy(chunk, block, 1).wait_send()
+
+
+def column_tiles(width, tile):
+    return [(start, min(tile, width - start)) for start in range(0, width, tile)]
+
+
+def mlp_kernel(
+    forward,
+    n,
+    own,
+    weights,
+    saved_in,
+    whole_out,
+    saved_out,
+    result,
+    whole,
+    w_vmem,
+    loaded,
+    stored,
+    partner,
+    arrived,
+    total,
+    held,
+    gather_send,
+    gather_recv,
+    pair_send,
+    pair_recv,
+    scatter_send,
+    scatter_recv,
+    own_sem,
+    w_sem,
+    load_sem,
+    store_sem,
+    whole_sem,
+):
+    chunks, rows, width = own.shape
+    hidden = w_vmem[0].shape[1]
+    line_rows = n * rows
+    all_rows = 2 * line_rows
+    gather = RowGather(n, own, whole, gather_send, gather_recv)
+    scatter = RowScatter(n, total, held, scatter_send, scatter_recv)
+    core = gather.core
+
+    w_copies = [
+        pltpu.make_async_copy(w, v, w_sem.at[i]) for i, (w, v) in enumerate(zip(weights, w_vmem))
+    ]
+    for copy in w_copies:
+        copy.start()
+    neighbour_barrier(n, gather.at, gather.up, gather.down, gather.sibling)
+    gather.begin(0)
+    own_copies = [
+        pltpu.make_async_copy(own.at[c], whole.at[c, core * n + gather.at], own_sem.at[c])
+        for c in range(chunks)
+    ]
+    for copy in own_copies:
+        copy.start()
+
+    def load(chunk, slot):
+        return [
+            pltpu.make_async_copy(ref.at[chunk], buf.at[slot], load_sem.at[i, slot])
+            for i, (ref, buf) in enumerate(zip(saved_in, loaded))
+        ]
+
+    def store(chunk, slot):
+        return [
+            pltpu.make_async_copy(buf.at[slot], ref.at[chunk], store_sem.at[i, slot])
+            for i, (ref, buf) in enumerate(zip(saved_out, stored))
+        ]
+
+    def keep(chunk):
+        return pltpu.make_async_copy(whole.at[chunk], whole_out.at[chunk], whole_sem.at[chunk])
+
+    def swap(chunk, slot):
+        return pltpu.make_async_remote_copy(
+            src_ref=partner.at[slot],
+            dst_ref=arrived.at[chunk],
+            send_sem=pair_send.at[slot],
+            recv_sem=pair_recv.at[chunk],
+            device_id=gather.sibling,
+            device_id_type=MESH,
+        )
+
+    for copy in load(0, 0):
+        copy.start()
+    for hop in range(1, n):
+        gather.step(0, hop)
+    for copy in own_copies + w_copies:
+        copy.wait()
+    gather.finish(0)
+
+    def pair_sum(chunk):
+        swap(chunk, 0).wait_recv()
+        for block in range(n):
+            total[chunk, block] = (
+                total[chunk, block].astype(jnp.float32)
+                + arrived[chunk, block].astype(jnp.float32)
+            ).astype(jnp.bfloat16)
+
+    def finish_chunk(chunk):
+        def write(value):
+            result[chunk] = value
+
+        scatter.finish(chunk, write)
+
+    tiles = column_tiles(hidden, 256)
+    groups = [tiles[: len(tiles) // 2], tiles[len(tiles) // 2 :]]
+
+    @pl.loop(0, chunks)
+    def _(chunk):
+        slot = lax.rem(chunk, 2)
+        more = chunk + 1 < chunks
+        behind = chunk > 0
+
+        keep(chunk).start()
+        for copy in load(chunk, slot):
+            copy.wait()
+
+        @pl.when(more)
+        def _():
+            gather.begin(chunk + 1)
+            for copy in load(chunk + 1, 1 - slot):
+                copy.start()
+
+        @pl.when(chunk > 1)
+        def _():
+            for copy in store(chunk, slot):
+                copy.wait()
+
+        def first_half(part):
+            for start, size in groups[part]:
+                cols = slice(start, start + size)
+                tokens = whole[chunk].reshape(all_rows, width)
+                if forward:
+                    gate = jnp.dot(tokens, w_vmem[0][:, cols], preferred_element_type=jnp.float32)
+                    up = jnp.dot(tokens, w_vmem[1][:, cols], preferred_element_type=jnp.float32)
+                    inner = gelu_scale * (gate + gelu_cubic * gate * gate * gate)
+                    wave = jnp.tanh(inner)
+                    half = 0.5 * (1.0 + wave)
+                    gelu = gate * half
+                    slope = half + 0.5 * gate * (1.0 - wave * wave) * gelu_scale * (
+                        1.0 + 3.0 * gelu_cubic * gate * gate
+                    )
+                    stored[0][slot, :, cols] = (gelu * up).astype(jnp.bfloat16)
+                    stored[1][slot, :, cols] = gelu.astype(jnp.bfloat16)
+                    stored[2][slot, :, cols] = (slope * up).astype(jnp.bfloat16)
+                else:
+                    dact = jnp.dot(tokens, w_vmem[2][:, cols], preferred_element_type=jnp.float32)
+                    stored[0][slot, :, cols] = (
+                        dact * loaded[1][slot, :, cols].astype(jnp.float32)
+                    ).astype(jnp.bfloat16)
+                    stored[1][slot, :, cols] = (
+                        dact * loaded[0][slot, :, cols].astype(jnp.float32)
+                    ).astype(jnp.bfloat16)
+
+        def second_half(line, put):
+            part = pl.ds(pl.multiple_of(line * line_rows, line_rows), line_rows)
+            for start, size in column_tiles(width, 768):
+                cols = slice(start, start + size)
+
+                def back(left, right):
+                    return lax.dot_general(
+                        left[slot, part, :],
+                        right[cols, :],
+                        (((1,), (1,)), ((), ())),
+                        preferred_element_type=jnp.float32,
+                    )
+
+                if forward:
+                    value = back(stored[0], w_vmem[2])
+                else:
+                    value = back(stored[0], w_vmem[0]) + back(stored[1], w_vmem[1])
+                put(cols, value.astype(jnp.bfloat16).reshape(n, rows, size))
+
+        def between(step):
+            @pl.when(more)
+            def _():
+                if step < n:
+                    gather.step(chunk + 1, step)
+                else:
+                    gather.finish(chunk + 1)
+
+            @pl.when(behind)
+            def _():
+                if step < n:
+                    scatter.step(chunk - 1, step)
+                else:
+                    finish_chunk(chunk - 1)
+
+        @pl.when(behind)
+        def _():
+            pair_sum(chunk - 1)
+
+        waits = list(range(1, n + 1))
+        first_half(0)
+        between(waits.pop(0))
+        first_half(1)
+        for copy in store(chunk, slot):
+            copy.start()
+        if len(waits) > 1:
+            between(waits.pop(0))
+
+        @pl.when(chunk > 1)
+        def _():
+            swap(chunk, slot).wait_send()
+
+        def put_partner(cols, value):
+            partner[slot, :, :, cols] = value
+
+        second_half(1 - core, put_partner)
+        while len(waits) > 1:
+            between(waits.pop(0))
+        swap(chunk, slot).start()
+
+        def put_total(cols, value):
+            total[chunk, :, :, cols] = value
+
+        second_half(core, put_total)
+        between(waits.pop(0))
+
+    last = chunks - 1
+    pair_sum(last)
+    for wave in range(1, n):
+        scatter.step(last, wave)
+    finish_chunk(last)
+
+    for chunk in range(chunks):
+        gather.drain(chunk)
+        scatter.drain(chunk)
+        keep(chunk).wait()
+    for chunk in range(max(chunks - 2, 0), chunks):
+        swap(chunk, chunk % 2).wait_send()
+        for copy in store(chunk, chunk % 2):
+            copy.wait()
+
+
+def mlp_half(forward, n, own, weights, saved, collective_id):
+    chunks, rows, width = own.shape
+    hidden = weights[0].shape[1]
+    all_rows = 2 * n * rows
+    outs = 3 if forward else 2
+    hidden_shape = jax.ShapeDtypeStruct((chunks, all_rows, hidden), jnp.bfloat16)
+
+    def kernel(*refs):
+        refs = list(refs)
+
+        def take(count):
+            taken = refs[:count]
+            del refs[:count]
+            return taken
+
+        (own_ref,) = take(1)
+        weight_refs = take(3)
+        saved_refs = take(len(saved))
+        (whole_out,) = take(1)
+        saved_out = take(outs)
+        (result,) = take(1)
+        (whole,) = take(1)
+        w_vmem = take(3)
+        loaded = take(len(saved))
+        stored = take(outs)
+        mlp_kernel(
+            forward,
+            n,
+            own_ref,
+            weight_refs,
+            saved_refs,
+            whole_out,
+            saved_out,
+            result,
+            whole,
+            w_vmem,
+            loaded,
+            stored,
+            *refs,
+        )
+
+    hbm = pl.BlockSpec(memory_space=pl.ANY)
+    vmem = pl.BlockSpec(memory_space=pltpu.VMEM)
+    bf16 = jnp.bfloat16
+    flops = 2 * chunks * all_rows * width * hidden * 3
+    return pl.pallas_call(
+        kernel,
+        name="mlp_forward" if forward else "mlp_backward",
+        out_shape=(
+            [jax.ShapeDtypeStruct((chunks, 2 * n, rows, width), bf16)]
+            + [hidden_shape] * outs
+            + [jax.ShapeDtypeStruct((chunks, rows, width), jnp.float32)]
+        ),
+        in_specs=[vmem] + [hbm] * (3 + len(saved)),
+        out_specs=[hbm] * (1 + outs) + [vmem],
+        scratch_shapes=(
+            [pltpu.VMEM((chunks, 2 * n, rows, width), bf16)]
+            + [pltpu.VMEM((width, hidden), bf16)] * 3
+            + [pltpu.VMEM((2, all_rows, hidden), bf16)] * (len(saved) + outs)
+            + [
+                pltpu.VMEM((2, n, rows, width), bf16),
+                pltpu.VMEM((chunks, n, rows, width), bf16),
+                pltpu.VMEM((chunks, n, rows, width), bf16),
+                pltpu.VMEM((chunks, n + 1, rows, width), bf16),
+                pltpu.SemaphoreType.DMA((chunks, 3, n)),
+                pltpu.SemaphoreType.DMA((chunks, 2 * n)),
+                pltpu.SemaphoreType.DMA((2,)),
+                pltpu.SemaphoreType.DMA((chunks,)),
+                pltpu.SemaphoreType.DMA((chunks, 2, n)),
+                pltpu.SemaphoreType.DMA((chunks, n + 1)),
+                pltpu.SemaphoreType.DMA((chunks,)),
+                pltpu.SemaphoreType.DMA((3,)),
+                pltpu.SemaphoreType.DMA((max(len(saved), 1), 2)),
+                pltpu.SemaphoreType.DMA((outs, 2)),
+                pltpu.SemaphoreType.DMA((chunks,)),
+            ]
+        ),
+        compiler_params=pltpu.CompilerParams(
+            collective_id=collective_id, has_side_effects=True, vmem_limit_bytes=60 << 20
+        ),
+        cost_estimate=pl.CostEstimate(
+            flops=flops, bytes_accessed=2 * 3 * width * hidden, transcendentals=0
+        ),
+    )(own, *weights, *saved)
+
+
+def on_device(
+    sizes,
+    block_in,
+    cotangent,
+    attention_matrix,
+    attention_first_moment,
+    attention_second_moment,
+    mlp_weight,
+    first_mlp,
+    second_mlp,
+    norm_weight,
+    first_norm,
+    second_norm,
+):
+    n_fsdp, n_seq, n_mlp = sizes
+    count = n_fsdp * n_seq * n_mlp
+    sequence_count, token_length, feat_width = block_in.shape
+    row_count = sequence_count * token_length
+    seq_rows = n_seq * row_count
+    query_total_width = QUERY_HEADS * HEAD_SIZE
+    key_value_width = KEY_VALUE_HEADS * HEAD_SIZE
+    group = QUERY_HEADS // KEY_VALUE_HEADS
+    heads = QUERY_HEADS // n_seq
+    kv_heads = KEY_VALUE_HEADS // n_seq
+    own_q = heads * HEAD_SIZE
+    own_kv = kv_heads * HEAD_SIZE
+    own_width = own_q + 2 * own_kv
+    share = attention_matrix.shape[0]
+
+    tok_rows = block_in.reshape(row_count, feat_width)
+    upstream = cotangent.reshape(row_count, feat_width)
+
+    gain_tile = jnp.zeros((1, 8, 128), jnp.float32)
+    gain_tile = gain_tile.at[0, : norm_weight.shape[0], : norm_weight.shape[1]].set(
+        norm_weight.astype(jnp.bfloat16).astype(jnp.float32)
+    )
+    gain_tiles = exchange(sizes, gain_tile, 0)
+    gains = gain_tiles[:, : norm_weight.shape[0], : norm_weight.shape[1]]
+    factor = 1.0 + jnp.transpose(gains, (1, 0, 2)).reshape(norm_weight.shape[0], feat_width)
+
+    attn_bf = attention_matrix.astype(jnp.bfloat16)
+    head_parts = jnp.concatenate(
+        [
+            attn_bf[:, :query_total_width].reshape(share, n_seq, own_q),
+            attn_bf[:, query_total_width : query_total_width + key_value_width].reshape(
+                share, n_seq, own_kv
+            ),
+            attn_bf[
+                :, query_total_width + key_value_width : query_total_width + 2 * key_value_width
+            ].reshape(share, n_seq, own_kv),
+        ],
+        axis=2,
+    )
+    head_cols = lax.all_to_all(
+        jnp.transpose(head_parts, (1, 0, 2)), "seq", split_axis=0, concat_axis=0, tiled=True
+    )
+    w_qkv = lax.all_gather(head_cols, ("fsdp", "mlp"), axis=0, tiled=False)
+    w_qkv = jnp.transpose(
+        w_qkv.reshape(n_fsdp, n_mlp, n_seq, share, own_width), (0, 2, 1, 3, 4)
+    ).reshape(feat_width, own_width)
+    w_out = lax.all_gather(
+        attn_bf[:, query_total_width + 2 * key_value_width :], AXES, axis=0, tiled=True
+    )
+
+    inverse_in = scale_rows(tok_rows)
+    normed_in = (tok_rows * inverse_in * factor[0]).astype(jnp.bfloat16)
+    whole_xn = lax.all_gather(normed_in, "seq", axis=0, tiled=True)
+    qkv = jnp.dot(whole_xn, w_qkv, preferred_element_type=jnp.float32).astype(jnp.bfloat16)
+    query_h = qkv[:, :own_q].reshape(sequence_count, seq_rows, heads, HEAD_SIZE)
+    key_h = jnp.repeat(
+        qkv[:, own_q : own_q + own_kv].reshape(sequence_count, seq_rows, kv_heads, HEAD_SIZE),
+        group,
+        axis=2,
+    )
+    value_h = jnp.repeat(
+        qkv[:, own_q + own_kv :].reshape(sequence_count, seq_rows, kv_heads, HEAD_SIZE),
+        group,
+        axis=2,
+    )
+    block_rows = min(512, seq_rows)
+    mixed_h, totals, saved_state = attend(query_h, key_h, value_h, block_rows)
+    mixed_rows = lax.all_to_all(
+        mixed_h.reshape(seq_rows, own_q), "seq", split_axis=0, concat_axis=1, tiled=True
+    )
+    projected = jnp.einsum("rc,dc->rd", mixed_rows, w_out, preferred_element_type=jnp.float32)
+    inverse_one = scale_rows(projected)
+    middle = tok_rows + projected * inverse_one * factor[1]
+    inverse_two = scale_rows(middle)
+    normed_mid = (middle * inverse_two * factor[2]).astype(jnp.bfloat16)
+    whole_mlp = lax.all_gather(mlp_weight.astype(jnp.bfloat16), "fsdp", axis=1, tiled=True)
+    mlp_parts = (whole_mlp[0], whole_mlp[1], whole_mlp[2])
+    chunk_shape = (mlp_chunks, row_count // mlp_chunks, feat_width)
+    hidden = whole_mlp.shape[2]
+    mlp_rows, hidden_activation, gelu_rows, slope_rows, ffn_out = mlp_half(
+        True, n_seq, normed_mid.reshape(chunk_shape), mlp_parts, (), 2
+    )
+    ffn_out = ffn_out.reshape(row_count, feat_width)
+    inverse_three = scale_rows(ffn_out)
+    block_out = middle + ffn_out * inverse_three * factor[3]
+    dffn, gain_three = norm_back(ffn_out, inverse_three, factor[3], upstream)
+    dffn_rows, gate_gradient, up_gradient_half, dnormed_mid = mlp_half(
+        False,
+        n_seq,
+        dffn.astype(jnp.bfloat16).reshape(chunk_shape),
+        mlp_parts,
+        (gelu_rows, slope_rows),
+        3,
+    )
+    dnormed_mid = dnormed_mid.reshape(row_count, feat_width)
+    mlp_rows = mlp_rows.reshape(-1, feat_width)
+    dffn_rows = dffn_rows.reshape(-1, feat_width)
+    hidden_activation = hidden_activation.reshape(-1, hidden)
+    gate_gradient = gate_gradient.reshape(-1, hidden)
+    up_gradient_half = up_gradient_half.reshape(-1, hidden)
+    grad_gate = jnp.einsum("rd,rf->df", mlp_rows, gate_gradient, preferred_element_type=jnp.float32)
+    grad_up = jnp.einsum(
+        "rd,rf->df", mlp_rows, up_gradient_half, preferred_element_type=jnp.float32
+    )
+    grad_down = jnp.einsum(
+        "rd,rf->df", dffn_rows, hidden_activation, preferred_element_type=jnp.float32
+    )
+    mlp_grad = lax.psum_scatter(
+        jnp.stack([grad_gate, grad_up, grad_down]).astype(jnp.bfloat16),
+        "fsdp",
+        scatter_dimension=1,
+        tiled=True,
+    ).astype(jnp.float32)
+    dmid_part, gain_two = norm_back(middle, inverse_two, factor[2], dnormed_mid)
+    dmiddle = upstream + dmid_part
+    dproj, gain_one = norm_back(projected, inverse_one, factor[1], dmiddle)
+    dproj_bf = dproj.astype(jnp.bfloat16)
+    dmixed = jnp.dot(dproj_bf, w_out, preferred_element_type=jnp.float32).astype(jnp.bfloat16)
+    dmixed_h = lax.all_to_all(dmixed, "seq", split_axis=1, concat_axis=0, tiled=True).reshape(
+        sequence_count, seq_rows, heads, HEAD_SIZE
+    )
+    grad_out = jnp.einsum("tr,tc->rc", dproj_bf, mixed_rows, preferred_element_type=jnp.float32)
+    grad_out = lax.psum_scatter(
+        grad_out.astype(jnp.bfloat16), AXES, scatter_dimension=0, tiled=True
+    ).astype(jnp.float32)
+    dquery_h, dkey_h, dvalue_h = attend_back(
+        query_h, key_h, value_h, mixed_h, totals, dmixed_h, block_rows
+    )
+
+    def group_sum(values):
+        return (
+            jnp.sum(
+                values.astype(jnp.float32).reshape(seq_rows, kv_heads, group, HEAD_SIZE), axis=2
+            )
+            .astype(jnp.bfloat16)
+            .reshape(seq_rows, own_kv)
+        )
+
+    dqkv = jnp.concatenate(
+        [dquery_h.reshape(seq_rows, own_q), group_sum(dkey_h), group_sum(dvalue_h)], axis=1
+    )
+    dnormed_in = lax.psum_scatter(
+        jnp.einsum("rc,dc->rd", dqkv, w_qkv, preferred_element_type=jnp.float32).astype(
+            jnp.bfloat16
+        ),
+        "seq",
+        scatter_dimension=0,
+        tiled=True,
+    ).astype(jnp.float32)
+    grad_qkv = jnp.einsum("tr,tc->rc", whole_xn, dqkv, preferred_element_type=jnp.float32)
+    grad_qkv = jnp.transpose(
+        grad_qkv.astype(jnp.bfloat16).reshape(n_fsdp, n_seq, n_mlp, share, own_width),
+        (0, 2, 1, 3, 4),
+    ).reshape(feat_width, own_width)
+    grad_qkv = lax.psum_scatter(grad_qkv, ("fsdp", "mlp"), scatter_dimension=0, tiled=True)
+    grad_qkv = jnp.transpose(
+        lax.all_to_all(
+            grad_qkv.reshape(n_seq, share, own_width),
+            "seq",
+            split_axis=0,
+            concat_axis=0,
+            tiled=True,
+        ),
+        (1, 0, 2),
+    ).astype(jnp.float32)
+    attn_grad = jnp.concatenate(
+        [
+            grad_qkv[:, :, :own_q].reshape(share, query_total_width),
+            grad_qkv[:, :, own_q : own_q + own_kv].reshape(share, key_value_width),
+            grad_qkv[:, :, own_q + own_kv :].reshape(share, key_value_width),
+            grad_out,
+        ],
+        axis=1,
+    )
+    dinput_part, gain_zero = norm_back(tok_rows, inverse_in, factor[0], dnormed_in)
+    input_grad = dmiddle + dinput_part
+
+    gain_sums = jnp.stack([gain_zero, gain_one, gain_two, gain_three])
+    gain_parts = jnp.transpose(gain_sums.reshape(4, count, feat_width // count), (1, 0, 2))
+    gain_parts = jnp.pad(gain_parts, ((0, 0), (0, 4), (0, 128 - feat_width // count)))
+    norm_grad = jnp.sum(exchange(sizes, gain_parts, 1), axis=0)[
+        : norm_weight.shape[0], : norm_weight.shape[1]
+    ]
+
+    attn_new, first_attn_new, second_attn_new = adam_update(
+        attention_matrix, attn_grad, attention_first_moment, attention_second_moment, decay_rate
+    )
+    mlp_new, first_mlp_new, second_mlp_new = adam_update(
+        mlp_weight, mlp_grad, first_mlp, second_mlp, decay_rate
+    )
+    norm_new, first_norm_new, second_norm_new = adam_update(
+        norm_weight, norm_grad, first_norm, second_norm, 0.0
+    )
+    return (
+        block_out.reshape(block_in.shape),
+        input_grad.reshape(block_in.shape),
+        attn_grad,
+        attn_new,
+        first_attn_new,
+        second_attn_new,
+        mlp_grad,
+        mlp_new,
+        first_mlp_new,
+        second_mlp_new,
+        norm_grad,
+        norm_new,
+        first_norm_new,
+        second_norm_new,
+    )
+
+
 def solution(mesh):
+    sizes = (mesh.shape["fsdp"], mesh.shape["seq"], mesh.shape["mlp"])
+    fits = KEY_VALUE_HEADS % sizes[1] == 0 and sizes[2] == 2
+    body = functools.partial(on_device, sizes) if fits else on_device_generic
     placed = (
         P(("fsdp", "mlp"), "seq", None),
         P(("fsdp", "mlp"), "seq", None),
@@ -350,7 +1165,7 @@
         P(None, ("fsdp", "seq", "mlp")),
     )
     return jax.shard_map(
-        on_device,
+        body,
         mesh=mesh,
         in_specs=placed,
         out_specs=(

time: 1480 us -> 1340 us (0.905)
  Pallas kernels: 0 us -> 356 us
  waiting for transfers between devices: 889 us -> 641 us
  blocking collectives: 149 us -> 22.3 us
  matrix products: 243 us -> 128 us
    pallas_call x0 -> x4, Pallas kernels: none -> 356 us  [the longest x2 331 us: mlp_half(): pl.pallas_call(kernel, name='mlp_forward' if forward else 'mlp_backward',...]
    all_gather x7 -> x3, waiting for transfers between devices: 372 us -> 106 us  [the longest x1 86.2 us: on_device(): whole_xn = lax.all_gather(normed_in, 'seq', axis=0, tiled=True)]
    reduce_scatter x1, waiting for transfers between devices: 0.01 us -> 142 us  [on_device(): lax.psum_scatter(jnp.stack([grad_gate, grad_up, grad_down]).astype(jnp.bf...]
    all_gather x1, waiting for transfers between devices: 0.02 us -> 140 us  [on_device(): lax.all_gather(mlp_weight.astype(jnp.bfloat16), 'fsdp', axis=1, tiled=True)]
    reduce_scatter x3, waiting for transfers between devices: 297 us -> 160 us  [the longest x1 117 us: on_device(): lax.psum_scatter(grad_out.astype(jnp.bfloat16), AXES, scatter_dimension=0...]
    all_to_all x6 -> x3, waiting for transfers between devices: 219 us -> 92.6 us  [the longest x1 48.1 us: on_device(): lax.all_to_all(mixed_h.reshape(seq_rows, own_q), 'seq', split_axis=0, con...]
    dot_general x9 -> x3, matrix products: 145 us -> 22.7 us  [the longest x1 9.3 us: on_device(): jnp.einsum('tr,tc->rc', whole_xn, dqkv, preferred_element_type=jnp.float32)]
    all_gather x1 -> x0, blocking collectives: 44.5 us -> none  [on_device(): lax.all_gather(norm_weight.astype(jnp.bfloat16), ('fsdp', 'seq', 'mlp'),...]
  transfers between devices with their start and end apart: 18 -> 11, of which waited for: 13 -> 10; matrix products, arithmetic and copies ran while one was open for 17% -> 11% of each run, Pallas kernels for 0% -> 2%
where the time goes in v1:
time: 1340 us; the launch traced here: 1330 us
  waiting for transfers between devices  641 us (48%)
  Pallas kernels  356 us (27%)
  matrix products  128 us (10%)
  other arithmetic  82.4 us (6%)
  local copies, waits for them, and re-layouts  60.8 us (5%)
  starting transfers between devices  23.6 us (2%)
  blocking collectives  22.3 us (2%)
  between operations  14.9 us (1%)
    pallas_call x2, Pallas kernels, mlp_half(): pl.pallas_call(kernel, name='mlp_forward' if forward else 'mlp_backward',...  331 us
    reduce_scatter x1, waiting for transfers between devices, on_device(): lax.psum_scatter(jnp.stack([grad_gate, grad_up, grad_down]).astype(jnp.bf...  142 us
    all_gather x1, waiting for transfers between devices, on_device(): lax.all_gather(mlp_weight.astype(jnp.bfloat16), 'fsdp', axis=1, tiled=True)  140 us
    reduce_scatter x1, waiting for transfers between devices, on_device(): lax.psum_scatter(grad_out.astype(jnp.bfloat16), AXES, scatter_dimension=0...  117 us
    all_gather x1, waiting for transfers between devices, on_device(): whole_xn = lax.all_gather(normed_in, 'seq', axis=0, tiled=True)  86.2 us
    all_to_all x1, waiting for transfers between devices, on_device(): lax.all_to_all(mixed_h.reshape(seq_rows, own_q), 'seq', split_axis=0, con...  48.1 us
    reduce_scatter x1, waiting for transfers between devices, on_device(): lax.psum_scatter(jnp.einsum('rc,dc->rd', dqkv, w_qkv, preferred_element_t...  42.2 us
    all_to_all x1, waiting for transfers between devices, on_device(): lax.all_to_all(grad_qkv.reshape(n_seq, share, own_width), 'seq', split_ax...  28.4 us
  transfers between devices with their start and end apart: 11, of which 10 were waited for; matrix products, arithmetic and copies ran while one was open for 11% of the time, Pallas kernels for 2%

profile of v1, /device:TPU:0, one launch (start us, length us, event | category | flops | bytes accessed | tf_op | source)
XLA Modules:
  0.0 1329.6 jit_solution(5140650568983194056)
XLA Ops:
  7.2 1.6 convert_element_type.159
  10.5 22.3 %all_to_all.45 = bf16[4,72,1024]{2,1,0:T(8,128)(2,1)} all-to-all(bf16[4,72,1024]{2,1,0:T(8,128)(2,1)S(1)} %copy.92), channel_id=1, replica_groups=mesh['fsdp'=4,'seq'=4,'mlp'=2] {'seq'}, dimensions={0} | all-to-all | bytes 1179648 | tf_op jit(solution)/shard_map/all_to_all | solution.py:978
  33.4 10.7 shard_map.218
  47.8 5.6 convert_element_type.162
  53.4 17.4 %all-gather.12.cloned.1.call-done = bf16[32,72,1024]{2,1,0:T(8,128)(2,1)} async-done(((bf16[4,72,1024]{2,1,0:T(8,128)(2,1)}), bf16[32,72,1024]{2,1,0:T(8,128)(2,1)}) %all-gather.12.cloned.1.call-update) | async-done | bytes 4718608 | tf_op jit(solution)/shard_map/all_gather | solution.py:981
  70.8 5.3 copy.93
  76.1 86.2 %all-gather.6.cloned.1.call-done = bf16[1024,2304]{1,0:T(8,128)(2,1)} async-done(((bf16[256,2304]{1,0:T(8,128)(2,1)}), bf16[1024,2304]{1,0:T(8,128)(2,1)}) %all-gather.6.cloned.1.call-update) | async-done | bytes 4718608 | tf_op jit(solution)/shard_map/all_gather | solution.py:991
  162.4 8.4 convolution_convert_fusion.8
  173.9 1.5 copy.94
  175.4 1.5 broadcast.309.clone
  176.9 12.4 while.39
  177.3 2.9 select_reduce_fusion.2
  183.5 2.9 select_reduce_fusion.2
  189.3 2.5 all_to_all.33
  191.8 14.7 %all-to-all-start.1 = ((bf16[4,256,512]{2,1,0:T(8,128)(2,1)}), bf16[4,256,512]{2,1,0:T(8,128)(2,1)}, u32[]{:S(2)}, u32[]{:S(2)}) async-start(bf16[4,256,512]{2,1,0:T(8,128)(2,1)} %all_to_all.33), calls=%async_computation.1 | async-start | bytes 2097152 | tf_op jit(solution)/shard_map/all_to_all | solution.py:1006
  206.8 48.1 %all-to-all-done.1 = bf16[4,256,512]{2,1,0:T(8,128)(2,1)} async-done(((bf16[4,256,512]{2,1,0:T(8,128)(2,1)}), bf16[4,256,512]{2,1,0:T(8,128)(2,1)}, u32[]{:S(2)}, u32[]{:S(2)}) %all-to-all-start.1) | async-done | bytes 1048608 | tf_op jit(solution)/shard_map/all_to_all | solution.py:1006
  254.9 2.3 copy.98
  257.2 2.8 all-gather.8.cloned.1.call-done
  260.0 6.8 multiply_reduce_fusion.5
  268.2 1.5 copy-done.3
  271.0 140.1 %all-gather.10.cloned.1.call-done = bf16[3,2304,1152]{2,1,0:T(8,128)(2,1)} async-done(((bf16[3,576,1152]{2,1,0:T(8,128)(2,1)}), bf16[3,2304,1152]{2,1,0:T(8,128)(2,1)}) %all-gather.10.cloned.1.call-update) | async-done | bytes 15925264 | tf_op jit(solution)/shard_map/all_gather | solution.py:1014
  411.1 12.1 slice_bitcast_fusion
  423.2 166.6 %mlp_forward.1 = (bf16[4,8,64,2304]{3,2,1,0:T(8,128)(2,1)}, bf16[4,512,1152]{2,1,0:T(8,128)(2,1)}, bf16[4,512,1152]{2,1,0:T(8,128)(2,1)}, bf16[4,512,1152]{2,1,0:T(8,128)(2,1)}, f32[4,64,2304]{2,1,0:T(8,128)}) custom-call(bf16[4,64,2304]{2,1,0:T(8,128)(2,1)} %bitcast.206, bf16[2304,1152]{1,0:T(8,128)(2,1)} %get-tuple-element.648.refs_1_, ...), custom_call_target="tpu_custom_call" | custom-call | flops 32614907904 | bytes 15925248 | tf_op jit(solution)/shard_map/mlp_forward/pallas_call | solution.py:884
  589.8 2.1 multiply_reduce_fusion.3
  592.1 5.1 fusion.59
  597.3 3.9 multiply_convert_fusion.2.refs_0_
  601.2 164.9 %mlp_backward.1 = (bf16[4,8,64,2304]{3,2,1,0:T(8,128)(2,1)}, bf16[4,512,1152]{2,1,0:T(8,128)(2,1)}, bf16[4,512,1152]{2,1,0:T(8,128)(2,1)}, f32[4,64,2304]{2,1,0:T(8,128)}) custom-call(bf16[4,64,2304]{2,1,0:T(8,128)(2,1)} %multiply_convert_fusion.2.refs_0_, bf16[2304,1152]{1,0:T(8,128)(2,1)} %get-tuple-element.648.refs_1_, ...), custom_call_target="tpu_custom_call" | custom-call | flops 32614907904 | bytes 15925248 | tf_op jit(solution)/shard_map/mlp_backward/pallas_call | solution.py:884
  766.1 3.1 fusion.56
  769.2 3.8 multiply_reduce_fusion
  774.5 2.8 convolution_convert_fusion.7
  778.3 4.5 all-to-all-start.2
  782.9 16.0 %all-to-all-done.2 = bf16[256,4,512]{2,0,1:T(8,128)(2,1)} async-done(((bf16[256,4,512]{2,0,1:T(8,128)(2,1)}), bf16[256,4,512]{2,0,1:T(8,128)(2,1)}, u32[]{:S(2)}, u32[]{:S(2)}) %all-to-all-start.2) | async-done | bytes 1048608 | tf_op jit(solution)/shard_map/all_to_all | solution.py:1057
  798.9 2.1 reshape.484
  801.0 3.8 multiply_reduce_fusion.6
  807.1 37.5 %while.40 = (s32[]{:T(128)}, bf16[1,1024,2,256]{1,3,2,0:T(8,128)(2,1)}, f32[1,1024,2,256]{1,3,2,0:T(8,128)S(1)}, f32[1,1024,2,256]{1,3,2,0:T(8,128)}, bf16[1,102...) while((s32[]{:T(128)}, ...), condition=%wide.region_12.13_spmd.clone, body=%wide.region_11.12_spmd.clone.sunk | while | flops 2704015872 | bytes 82346464 | solution.py:132
  807.1 2.2 fusion.111
  811.7 3.6 multiply_convert_fusion.6
  815.3 2.8 bitcast_add_fusion.8
  819.9 5.6 bitcast_add_fusion.9
  825.5 2.2 fusion.111
  830.1 3.6 multiply_convert_fusion.6
  833.7 2.8 bitcast_add_fusion.8
  838.3 6.3 bitcast_add_fusion.9
  844.6 2.1 convert_reduce_fusion
  846.8 9.3 convolution_convert_fusion.5
  856.1 2.7 copy.107
  860.0 9.1 convolution_convert_fusion.6
  871.0 5.1 convolution_convert_fusion.4
  876.1 16.9 %fusion.45 = bf16[1,2304,1152]{2,1,0:T(8,128)(2,1)S(1)} fusion(bf16[2048,2304]{1,0:T(8,128)(2,1)} %bitcast.213, bf16[2048,1152]{1,0:T(8,128)(2,1)} %bitcast.222), kind=kOutput, calls=%fused_computation.64 | convolution fusion | flops 10874290176 | bytes 19464192 | tf_op jit(solution)/shard_map/rd,rf->df/dot_general | solution.py:1039
  893.1 15.3 %fusion.46 = bf16[1,2304,1152]{2,1,0:T(8,128)(2,1)S(1)} fusion(bf16[2048,2304]{1,0:T(8,128)(2,1)S(1)} %bitcast.216, bf16[2048,1152]{1,0:T(8,128)(2,1)} %bitcast.221), kind=kOutput, calls=%fused_computation.65 | convolution fusion | flops 10874290176 | bytes 19464192 | tf_op jit(solution)/shard_map/rd,rf->df/dot_general | solution.py:1040
  908.4 15.2 %fusion.47 = bf16[1,2304,1152]{2,1,0:T(8,128)(2,1)S(1)} fusion(bf16[2048,2304]{1,0:T(8,128)(2,1)} %bitcast.217, bf16[2048,1152]{1,0:T(8,128)(2,1)S(1)} %bitcast.220), kind=kOutput, calls=%fused_computation.66 | convolution fusion | flops 10874290176 | bytes 19464192 | tf_op jit(solution)/shard_map/rd,rf->df/dot_general | solution.py:1043
  923.6 7.1 pad_maximum_fusion
  930.7 4.1 all-to-all-start.3
  936.9 28.4 %all-to-all-done.3 = bf16[4,72,1024]{2,1,0:T(8,128)(2,1)S(1)} async-done(((bf16[4,72,1024]{2,1,0:T(8,128)(2,1)}), bf16[4,72,1024]{2,1,0:T(8,128)(2,1)S(1)}, u32[]{:S(2)}, u32[]{:S(2)}) %all-to-all-start.3) | async-done | bytes 589856 | tf_op jit(solution)/shard_map/all_to_all | solution.py:1095
  968.0 42.2 %reduce-scatter.5.cloned.1.call-done = bf16[256,2304]{1,0:T(8,128)(2,1)} async-done(((bf16[1024,2304]{1,0:T(8,128)(2,1)}), bf16[256,2304]{1,0:T(8,128)(2,1)}) %reduce-scatter.5.cloned.1.call-update) | async-done | bytes 1179664 | tf_op jit(solution)/shard_map/reduce_scatter | solution.py:1080
  1010.2 2.8 fusion.55
  1013.0 1.4 stack.35
  1016.0 14.0 %shard_map.219 = f32[32,8,128]{2,1,0:T(8,128)} custom-call(f32[32,8,128]{2,1,0:T(8,128)} %pad.10.mine_ref), custom_call_target="tpu_custom_call" | custom-call | tf_op jit(solution)/shard_map/pallas_call | solution.py:391
  1029.9 1.5 reduce_sum.179
  1033.5 3.8 fusion.54
  1037.3 117.2 %reduce-scatter.9.cloned.1.call-done = bf16[72,2048]{1,0:T(8,128)(2,1)} async-done(((bf16[2304,2048]{1,0:T(8,128)(2,1)}), bf16[72,2048]{1,0:T(8,128)(2,1)}) %reduce-scatter.9.cloned.1.call-update) | async-done | bytes 294928 | tf_op jit(solution)/shard_map/reduce_scatter | solution.py:1061
  1155.6 6.3 multiply_subtract_fusion.1
  1161.9 142.0 %reduce-scatter.11.cloned.1.call-done = bf16[3,576,1152]{2,1,0:T(8,128)(2,1)} async-done(((bf16[3,2304,1152]{2,1,0:T(8,128)(2,1)}), bf16[3,576,1152]{2,1,0:T(8,128)(2,1)}) %reduce-scatter.11.cloned.1.call-update) | async-done | bytes 3981328 | tf_op jit(solution)/shard_map/reduce_scatter | solution.py:1046
  1303.9 18.7 %multiply_subtract_fusion = (f32[3,576,1152]{2,1,0:T(8,128)}, f32[3,576,1152]{2,1,0:T(8,128)}, f32[3,576,1152]{2,1,0:T(8,128)}, f32[3,576,1152]{2,1,0:T(8,128)}) fusion(f32[3,576,1152]{2,1,0:T(8,128)} %param.22, f32[3,576,1152]{2,1,0:T(8,128)} %param.23, f32[3,576,1152]{2,1,0:T(8,128)} %param.24, bf16[3,576,1152]{2,1,0:T(8,128)(2,1)} %reduce-scatter.11.cloned.1.call-done), kind=kLoop, calls=%fused_computation.68 | loop fusion | flops 31850496 | bytes 59719680 | tf_op jit(solution)/shard_map/sub | solution.py:49
  (214 shorter events, 44.1 us)
Async XLA Ops:
  7.2 63.6 %all-gather.12.cloned.1.call-start = ((), (), s32[]{:S(2)}) async-start(), calls=%async_computation.15 | async-start | bytes 5308416 | tf_op jit(solution)/shard_map/all_gather | solution.py:981
  9.8 23.0 %copy-start.36 = (f32[4,72]{1,0:T(4,128)S(1)}, f32[4,72]{1,0:T(4,128)}, u32[]{:S(2)}) copy-start(f32[4,72]{1,0:T(4,128)} %param.25) | copy-start | bytes 3460
  9.9 35.5 %copy-start.1 = (f32[1,256,2304]{2,1,0:T(8,128)S(1)}, f32[1,256,2304]{2,1,0:T(8,128)}, u32[]{:S(2)}) copy-start(f32[1,256,2304]{2,1,0:T(8,128)} %param.17) | copy-start | bytes 7077892
  32.8 129.6 %all-gather.6.cloned.1.call-start = ((), (), s32[]{:S(2)}) async-start(), calls=%async_computation.8 | async-start | bytes 5898240 | tf_op jit(solution)/shard_map/all_gather | solution.py:991
  45.4 1.5 copy-start.29
  45.6 1.3 copy-start.34
  47.0 213.0 %all-gather.8.cloned.1.call-start = ((), (), s32[]{:S(2)}) async-start(), calls=%async_computation.9 | async-start | bytes 9732096 | tf_op jit(solution)/shard_map/all_gather | solution.py:985
  47.7 363.4 %all-gather.10.cloned.1.call-start = ((), (), s32[]{:S(2)}) async-start(), calls=%async_computation.10 | async-start | bytes 19906560 | tf_op jit(solution)/shard_map/all_gather | solution.py:1014
  177.3 2.9 copy-start.27
  180.2 1.3 copy-start.16
  183.5 2.9 copy-start.27
  186.4 1.3 copy-start.16
  191.8 63.1 %all-to-all-start.1 = ((bf16[4,256,512]{2,1,0:T(8,128)(2,1)}), bf16[4,256,512]{2,1,0:T(8,128)(2,1)}, u32[]{:S(2)}, u32[]{:S(2)}) async-start(bf16[4,256,512]{2,1,0:T(8,128)(2,1)} %all_to_all.33), calls=%async_computation.1 | async-start | bytes 2097152 | tf_op jit(solution)/shard_map/all_to_all | solution.py:1006
  266.8 1.4 copy-start.9
  268.2 1.5 copy-start.3
  589.8 2.4 copy-start.4
  766.1 3.1 copy-start.10
  766.1 3.1 copy-start.11
  766.1 8.3 slice-start
  769.2 5.3 slice-start.1
  769.2 5.2 slice-start.2
  773.1 1.4 copy-start.8
  774.5 2.8 copy-start.18
  778.3 20.5 %all-to-all-start.2 = ((bf16[256,4,512]{2,0,1:T(8,128)(2,1)}), bf16[256,4,512]{2,0,1:T(8,128)(2,1)}, u32[]{:S(2)}, u32[]{:S(2)}) async-start(bf16[256,4,512]{2,0,1:T(8,128)(2,1)} %bitcast.164), calls=%async_computation.2 | async-start | bytes 2097152 | tf_op jit(solution)/shard_map/all_to_all | solution.py:1057
  782.9 147.9 %reduce-scatter.7.cloned.1.call-start = ((), (), s32[]{:S(2)}) async-start(), calls=%async_computation.12 | async-start | bytes 5308416 | tf_op jit(solution)/shard_map/reduce_scatter | solution.py:1093
  807.1 8.2 copy-start.6
  807.1 2.2 copy-start.12
  807.1 4.6 copy-start.28
  809.3 2.0 copy-start
  809.7 1.8 copy-start.15
  810.2 1.5 copy-start.14
  815.3 2.8 copy-start.5
  815.3 2.8 copy-start.13
  819.9 5.6 copy-start.7
  825.5 8.2 copy-start.6
  825.5 2.2 copy-start.12
  825.5 4.6 copy-start.28
  827.7 2.0 copy-start
  828.1 1.8 copy-start.15
  828.6 1.5 copy-start.14
  833.7 2.8 copy-start.5
  833.7 2.8 copy-start.13
  838.3 6.3 copy-start.7
  844.6 2.1 copy-start.22
  846.8 9.3 copy-start.23
  846.8 9.3 copy-start.25
  858.9 151.3 %reduce-scatter.5.cloned.1.call-start = ((), (), s32[]{:S(2)}) async-start(), calls=%async_computation.11 | async-start | bytes 5898240 | tf_op jit(solution)/shard_map/reduce_scatter | solution.py:1080
  869.2 1.4 copy-start.19
  869.2 1.8 copy-start.21
  869.2 285.4 %reduce-scatter.9.cloned.1.call-start = ((), (), s32[]{:S(2)}) async-start(), calls=%async_computation.13 | async-start | bytes 9732096 | tf_op jit(solution)/shard_map/reduce_scatter | solution.py:1061
  876.0 17.0 %slice-start.3 = ((s8[9437184]{0:T(1024)(128)(4,1)}), s8[1048576]{0:T(1024)(128)(4,1)S(1)}, s32[]{:S(2)}) async-start(s8[9437184]{0:T(1024)(128)(4,1)} %bitcast.214), calls=%async_computation.19 | async-start | bytes 2097152
  876.0 427.8 %reduce-scatter.11.cloned.1.call-start = ((), (), s32[]{:S(2)}) async-start(), calls=%async_computation.14 | async-start | bytes 19906560 | tf_op jit(solution)/shard_map/reduce_scatter | solution.py:1046
  876.1 16.9 %slice-start.4 = ((s8[9437184]{0:T(1024)(128)(4,1)}), s8[4194304]{0:T(1024)(128)(4,1)S(1)}, s32[]{:S(2)}) async-start(s8[9437184]{0:T(1024)(128)(4,1)} %bitcast.214), calls=%async_computation.20 | async-start | bytes 8388608
  876.1 16.9 %slice-start.5 = ((s8[9437184]{0:T(1024)(128)(4,1)}), s8[4194304]{0:T(1024)(128)(4,1)S(1)}, s32[]{:S(2)}) async-start(s8[9437184]{0:T(1024)(128)(4,1)} %bitcast.214), calls=%async_computation.21 | async-start | bytes 8388608
  876.1 32.2 %slice-start.6 = ((s8[4718592]{0:T(1024)(128)(4,1)}), s8[4194304]{0:T(1024)(128)(4,1)S(1)}, s32[]{:S(2)}) async-start(s8[4718592]{0:T(1024)(128)(4,1)} %bitcast.218), calls=%async_computation.22 | async-start | bytes 8388608
  893.1 15.3 %slice-start.7 = ((s8[4718592]{0:T(1024)(128)(4,1)}), s8[524288]{0:T(1024)(128)(4,1)S(1)}, s32[]{:S(2)}) async-start(s8[4718592]{0:T(1024)(128)(4,1)} %bitcast.218), calls=%async_computation.23 | async-start | bytes 1048576
  930.7 4.1 copy-start.32
  930.7 4.8 copy-start.33
  930.7 5.6 copy-start.31
  930.7 34.6 %all-to-all-start.3 = ((bf16[4,72,1024]{2,1,0:T(8,128)(2,1)}), bf16[4,72,1024]{2,1,0:T(8,128)(2,1)S(1)}, u32[]{:S(2)}, u32[]{:S(2)}) async-start(bf16[4,72,1024]{2,1,0:T(8,128)(2,1)} %bitcast.210), calls=%async_computation.5 | async-start | bytes 1179648 | tf_op jit(solution)/shard_map/all_to_all | solution.py:1095
  965.5 44.7 %copy-start.2 = (f32[1,256,2304]{2,1,0:T(8,128)S(1)}, f32[1,256,2304]{2,1,0:T(8,128)}, u32[]{:S(2)}) copy-start(f32[1,256,2304]{2,1,0:T(8,128)} %param.17) | copy-start | bytes 7077892
  965.5 44.7 %copy-start.30 = (f32[2304]{0:T(1024)S(1)}, f32[2304]{0:T(1024)}, u32[]{:S(2)}) copy-start(f32[2304]{0:T(1024)} %copy-done.29) | copy-start | bytes 27652
  965.5 44.7 %copy-start.35 = (f32[256]{0:T(256)S(1)}, f32[256]{0:T(256)}, u32[]{:S(2)}) copy-start(f32[256]{0:T(256)} %copy-done.34) | copy-start | bytes 3076
  1010.2 23.3 %copy-start.20 = (bf16[256,2304]{1,0:T(8,128)(2,1)S(1)}, bf16[256,2304]{1,0:T(8,128)(2,1)}, u32[]{:S(2)}) copy-start(bf16[256,2304]{1,0:T(8,128)(2,1)} %reduce-scatter.5.cloned.1.call-done) | copy-start | bytes 3538948
  (4 other events, 4.2 us)
Sparse Core Ops, SparseCore 0:
  32.9 37.8 all-gather.11
  72.9 89.3 all-gather.5
  166.0 93.9 all-gather.7
  262.2 148.8 all-gather.9
  859.0 53.6 reduce-scatter.6
  915.4 94.7 reduce-scatter.4
  1016.1 138.4 reduce-scatter.8
  1157.7 146.1 reduce-scatter.10

commit v2 on v1

--- a/solution.py
+++ b/solution.py
@@ -24,6 +24,7 @@
 gelu_scale = math.sqrt(2.0 / math.pi)
 gelu_cubic = 0.044715
 mlp_chunks = 4
+row_chunks = 2
 
 
 def scale_rows(values):
@@ -347,10 +348,21 @@
 AXES = ("fsdp", "seq", "mlp")
 
 
-def exchange_kernel(sizes, mine_ref, out_ref, send_sem, recv_sem):
+def exchange_kernel(
+    sizes,
+    mine_ref,
+    block_ref,
+    out_ref,
+    landed_ref,
+    send_sem,
+    recv_sem,
+    block_send,
+    block_recv,
+):
     n_fsdp, n_seq, n_mlp = sizes
     count = n_fsdp * n_seq * n_mlp
-    me = (lax.axis_index("fsdp") * n_seq + lax.axis_index("seq")) * n_mlp + lax.axis_index("mlp")
+    fsdp, at, core = lax.axis_index("fsdp"), lax.axis_index("seq"), lax.axis_index("mlp")
+    me = (fsdp * n_seq + at) * n_mlp + core
     slots = mine_ref.shape[0]
 
     def place(index):
@@ -363,6 +375,17 @@
         pl.semaphore_signal(barrier, inc=1, device_id=place((me + step) % count), device_id_type=MESH)
 
     pl.semaphore_wait(barrier, count - 1)
+
+    def block_to(step):
+        to = lax.rem(at + step, n_seq)
+        return pltpu.make_async_remote_copy(
+            src_ref=block_ref.at[to],
+            dst_ref=landed_ref.at[at],
+            send_sem=block_send.at[step],
+            recv_sem=block_recv.at[step],
+            device_id=(fsdp, to, core),
+            device_id_type=MESH,
+        )
 
     def copy_to(step):
         to = (me + step) % count
@@ -379,23 +402,41 @@
     def _(step):
         copy_to(step).start()
 
+    for step in range(1, n_seq):
+        block_to(step).start()
+    own = pltpu.make_async_copy(block_ref.at[at], landed_ref.at[at], block_send.at[0])
+    own.start()
     out_ref[pl.ds(me, 1)] = mine_ref[pl.ds(me % slots, 1)]
 
     @pl.loop(1, count)
     def _(step):
         copy_to(step).wait()
 
-
-def exchange(sizes, mine, collective_id):
+    for step in range(1, n_seq):
+        block_to(step).wait()
+    own.wait()
+
+
+def exchange(sizes, mine, blocks, collective_id):
     count = sizes[0] * sizes[1] * sizes[2]
+    vmem = pl.BlockSpec(memory_space=pltpu.VMEM)
     return pl.pallas_call(
         functools.partial(exchange_kernel, sizes),
-        out_shape=jax.ShapeDtypeStruct((count,) + mine.shape[1:], mine.dtype),
-        in_specs=[pl.BlockSpec(memory_space=pltpu.VMEM)],
-        out_specs=pl.BlockSpec(memory_space=pltpu.VMEM),
-        scratch_shapes=[pltpu.SemaphoreType.DMA((count,)), pltpu.SemaphoreType.DMA((count,))],
+        name="exchange",
+        out_shape=[
+            jax.ShapeDtypeStruct((count,) + mine.shape[1:], mine.dtype),
+            jax.ShapeDtypeStruct(blocks.shape, blocks.dtype),
+        ],
+        in_specs=[vmem, vmem],
+        out_specs=[vmem, vmem],
+        scratch_shapes=[
+            pltpu.SemaphoreType.DMA((count,)),
+            pltpu.SemaphoreType.DMA((count,)),
+            pltpu.SemaphoreType.DMA((sizes[1],)),
+            pltpu.SemaphoreType.DMA((sizes[1],)),
+        ],
         compiler_params=pltpu.CompilerParams(collective_id=collective_id, has_side_effects=True),
-    )(mine)
+    )(mine, blocks)
 
 
 def neighbour_barrier(seq_count, at, up, down, sibling):
@@ -417,8 +458,8 @@
 
 
 class RowGather:
-    def __init__(self, n, own, whole, send_sem, recv_sem):
-        self.n, self.own, self.whole = n, own, whole
+    def __init__(self, n, own, whole, send_sem, recv_sem, pair=True):
+        self.n, self.own, self.whole, self.pair = n, own, whole, pair
         self.send_sem, self.recv_sem = send_sem, recv_sem
         self.fsdp, self.at, self.core = (
             lax.axis_index("fsdp"),
@@ -428,12 +469,16 @@
         self.up = (self.fsdp, lax.rem(self.at + 1, n), self.core)
         self.down = (self.fsdp, lax.rem(self.at + n - 1, n), self.core)
         self.sibling = (self.fsdp, self.at, 1 - self.core)
+        self.base = self.core * n if pair else 0
+
+    def spot(self, chunk, slot):
+        return self.whole.at[chunk, slot] if self.pair else self.whole.at[slot, chunk]
 
     def copy(self, chunk, block, way, own=False):
-        slot = self.core * self.n + block
+        slot = self.base + block
         return pltpu.make_async_remote_copy(
-            src_ref=self.own.at[chunk] if own else self.whole.at[chunk, slot],
-            dst_ref=self.whole.at[chunk, slot],
+            src_ref=self.own.at[chunk] if own else self.spot(chunk, slot),
+            dst_ref=self.spot(chunk, slot),
             send_sem=self.send_sem.at[chunk, way, block],
             recv_sem=self.recv_sem.at[chunk, slot],
             device_id=(self.up, self.down, self.sibling)[way],
@@ -443,10 +488,10 @@
     def arrival(self, chunk, slot):
         return pltpu.make_async_remote_copy(
             src_ref=self.own.at[chunk],
-            dst_ref=self.whole.at[chunk, slot],
+            dst_ref=self.spot(chunk, slot),
             send_sem=self.send_sem.at[chunk, 0, 0],
             recv_sem=self.recv_sem.at[chunk, slot],
-            device_id=self.sibling,
+            device_id=self.sibling if self.pair else self.up,
             device_id_type=MESH,
         )
 
@@ -459,30 +504,33 @@
         def _():
             self.copy(chunk, self.at, 1, True).start()
 
-        self.copy(chunk, self.at, 2, True).start()
+        if self.pair:
+            self.copy(chunk, self.at, 2, True).start()
 
     def step(self, chunk, hop):
         below, above = self.at - hop, self.at + hop
 
         @pl.when(below >= 0)
         def _():
-            self.arrival(chunk, self.core * self.n + below).wait_recv()
+            self.arrival(chunk, self.base + below).wait_recv()
 
             @pl.when(self.at < self.n - 1)
             def _():
                 self.copy(chunk, below, 0).start()
 
-            self.copy(chunk, below, 2).start()
+            if self.pair:
+                self.copy(chunk, below, 2).start()
 
         @pl.when(above < self.n)
         def _():
-            self.arrival(chunk, self.core * self.n + above).wait_recv()
+            self.arrival(chunk, self.base + above).wait_recv()
 
             @pl.when(self.at > 0)
             def _():
                 self.copy(chunk, above, 1).start()
 
-            self.copy(chunk, above, 2).start()
+            if self.pair:
+                self.copy(chunk, above, 2).start()
 
     def finish(self, chunk):
         for block in range(self.n):
@@ -499,7 +547,8 @@
             def _():
                 self.copy(chunk, block, 1).wait_send()
 
-            self.copy(chunk, block, 2).wait_send()
+            if self.pair:
+                self.copy(chunk, block, 2).wait_send()
 
 
 class RowScatter:
@@ -922,6 +971,140 @@
     )(own, *weights, *saved)
 
 
+def gather_kernel(n, own, whole, send_sem, recv_sem, own_sem):
+    chunks = own.shape[0]
+    gather = RowGather(n, own, whole, send_sem, recv_sem, pair=False)
+    neighbour_barrier(n, gather.at, gather.up, gather.down, None)
+    for chunk in range(chunks):
+        gather.begin(chunk)
+    own_copies = [
+        pltpu.make_async_copy(own.at[c], gather.spot(c, gather.at), own_sem.at[c])
+        for c in range(chunks)
+    ]
+    for copy in own_copies:
+        copy.start()
+    for hop in range(1, n):
+        for chunk in range(chunks):
+            gather.step(chunk, hop)
+    for copy in own_copies:
+        copy.wait()
+    for chunk in range(chunks):
+        gather.drain(chunk)
+
+
+def gather_rows(n, own, collective_id):
+    chunks = own.shape[0]
+    vmem = pl.BlockSpec(memory_space=pltpu.VMEM)
+    return pl.pallas_call(
+        functools.partial(gather_kernel, n),
+        name="gather_rows",
+        out_shape=jax.ShapeDtypeStruct((n,) + own.shape, own.dtype),
+        in_specs=[vmem],
+        out_specs=vmem,
+        scratch_shapes=[
+            pltpu.SemaphoreType.DMA((chunks, 3, n)),
+            pltpu.SemaphoreType.DMA((chunks, n)),
+            pltpu.SemaphoreType.DMA((chunks,)),
+        ],
+        compiler_params=pltpu.CompilerParams(collective_id=collective_id, has_side_effects=True),
+    )(own)
+
+
+def multiply_scatter_kernel(
+    n, first, left, right, result, total, held, right_vmem, send_sem, recv_sem, right_sem
+):
+    chunks, rows, width = result.shape
+    depth = left.shape[3]
+    scatter = RowScatter(n, total, held, send_sem, recv_sem)
+    at, far = scatter.at, n - 1 - scatter.at
+    fetch = pltpu.make_async_copy(right, right_vmem, right_sem.at[0])
+    fetch.start()
+    neighbour_barrier(n, at, scatter.up, scatter.down, None)
+    fetch.wait()
+
+    def product(block, chunk, put):
+        for start, size in column_tiles(width, 768):
+            put(
+                slice(start, start + size),
+                lax.dot_general(
+                    left[block, chunk],
+                    right_vmem[start : start + size, first : first + depth],
+                    (((1,), (1,)), ((), ())),
+                    preferred_element_type=jnp.float32,
+                ),
+            )
+
+    def send(block, chunk, way, started):
+        def put(cols, value):
+            total[chunk, block, :, cols] = value.astype(jnp.bfloat16)
+
+        product(block, chunk, put)
+
+        @pl.when(started)
+        def _():
+            scatter.add(chunk, block)
+
+        scatter.copy(chunk, block, way).start()
+
+    @pl.loop(1, n)
+    def _(wave):
+        @pl.loop(0, chunks)
+        def _(chunk):
+            @pl.when(at < wave)
+            def _():
+                send(n - wave + at, chunk, 0, at > 0)
+
+            @pl.when(far < wave)
+            def _():
+                send(wave - 1 - far, chunk, 1, far > 0)
+
+    @pl.loop(0, chunks)
+    def _(chunk):
+        def put(cols, value):
+            result[chunk, :, cols] = value
+
+        product(at, chunk, put)
+
+    for chunk in range(chunks):
+
+        @pl.when(at > 0)
+        def _():
+            scatter.arrive(chunk, at)
+            result[chunk] += held[chunk, at].astype(jnp.float32)
+
+        @pl.when(far > 0)
+        def _():
+            scatter.arrive(chunk, n)
+            result[chunk] += held[chunk, n].astype(jnp.float32)
+
+        scatter.drain(chunk)
+
+
+def multiply_scatter(n, left, right, first, collective_id, name):
+    _, chunks, rows, depth = left.shape
+    width = right.shape[0]
+    vmem = pl.BlockSpec(memory_space=pltpu.VMEM)
+    hbm = pl.BlockSpec(memory_space=pl.ANY)
+    return pl.pallas_call(
+        functools.partial(multiply_scatter_kernel, n, first),
+        name=name,
+        out_shape=jax.ShapeDtypeStruct((chunks, rows, width), jnp.float32),
+        in_specs=[vmem, hbm],
+        out_specs=vmem,
+        scratch_shapes=[
+            pltpu.VMEM((chunks, n, rows, width), jnp.bfloat16),
+            pltpu.VMEM((chunks, n + 1, rows, width), jnp.bfloat16),
+            pltpu.VMEM(right.shape, right.dtype),
+            pltpu.SemaphoreType.DMA((chunks, 2, n)),
+            pltpu.SemaphoreType.DMA((chunks, n + 1)),
+            pltpu.SemaphoreType.DMA((1,)),
+        ],
+        compiler_params=pltpu.CompilerParams(
+            collective_id=collective_id, has_side_effects=True, vmem_limit_bytes=56 << 20
+        ),
+    )(left, right)
+
+
 def on_device(
     sizes,
     block_in,
@@ -958,38 +1141,30 @@
     gain_tile = gain_tile.at[0, : norm_weight.shape[0], : norm_weight.shape[1]].set(
         norm_weight.astype(jnp.bfloat16).astype(jnp.float32)
     )
-    gain_tiles = exchange(sizes, gain_tile, 0)
+    attn_bf = attention_matrix.astype(jnp.bfloat16)
+    own_o = query_total_width // n_seq
+    cuts = (query_total_width, key_value_width, key_value_width, query_total_width)
+    pieces, start = [], 0
+    for cut in cuts:
+        pieces.append(attn_bf[:, start : start + cut].reshape(share, n_seq, cut // n_seq))
+        start += cut
+    head_parts = jnp.transpose(jnp.concatenate(pieces, axis=2), (1, 0, 2))
+    gain_tiles, head_cols = exchange(sizes, gain_tile, head_parts, 0)
     gains = gain_tiles[:, : norm_weight.shape[0], : norm_weight.shape[1]]
     factor = 1.0 + jnp.transpose(gains, (1, 0, 2)).reshape(norm_weight.shape[0], feat_width)
-
-    attn_bf = attention_matrix.astype(jnp.bfloat16)
-    head_parts = jnp.concatenate(
-        [
-            attn_bf[:, :query_total_width].reshape(share, n_seq, own_q),
-            attn_bf[:, query_total_width : query_total_width + key_value_width].reshape(
-                share, n_seq, own_kv
-            ),
-            attn_bf[
-                :, query_total_width + key_value_width : query_total_width + 2 * key_value_width
-            ].reshape(share, n_seq, own_kv),
-        ],
-        axis=2,
-    )
-    head_cols = lax.all_to_all(
-        jnp.transpose(head_parts, (1, 0, 2)), "seq", split_axis=0, concat_axis=0, tiled=True
-    )
-    w_qkv = lax.all_gather(head_cols, ("fsdp", "mlp"), axis=0, tiled=False)
-    w_qkv = jnp.transpose(
-        w_qkv.reshape(n_fsdp, n_mlp, n_seq, share, own_width), (0, 2, 1, 3, 4)
-    ).reshape(feat_width, own_width)
-    w_out = lax.all_gather(
-        attn_bf[:, query_total_width + 2 * key_value_width :], AXES, axis=0, tiled=True
-    )
+    all_width = own_width + own_o
+    w_heads = lax.all_gather(head_cols, ("fsdp", "mlp"), axis=0, tiled=False)
+    w_heads = jnp.transpose(
+        w_heads.reshape(n_fsdp, n_mlp, n_seq, share, all_width), (0, 2, 1, 3, 4)
+    ).reshape(feat_width, all_width)
 
     inverse_in = scale_rows(tok_rows)
     normed_in = (tok_rows * inverse_in * factor[0]).astype(jnp.bfloat16)
-    whole_xn = lax.all_gather(normed_in, "seq", axis=0, tiled=True)
-    qkv = jnp.dot(whole_xn, w_qkv, preferred_element_type=jnp.float32).astype(jnp.bfloat16)
+    part_shape = (row_chunks, row_count // row_chunks, feat_width)
+    whole_xn = gather_rows(n_seq, normed_in.reshape(part_shape), 4).reshape(seq_rows, feat_width)
+    qkv = jnp.dot(
+        whole_xn, w_heads[:, :own_width], preferred_element_type=jnp.float32
+    ).astype(jnp.bfloat16)
     query_h = qkv[:, :own_q].reshape(sequence_count, seq_rows, heads, HEAD_SIZE)
     key_h = jnp.repeat(
         qkv[:, own_q : own_q + own_kv].reshape(sequence_count, seq_rows, kv_heads, HEAD_SIZE),
@@ -1003,10 +1178,15 @@
     )
     block_rows = min(512, seq_rows)
     mixed_h, totals, saved_state = attend(query_h, key_h, value_h, block_rows)
-    mixed_rows = lax.all_to_all(
-        mixed_h.reshape(seq_rows, own_q), "seq", split_axis=0, concat_axis=1, tiled=True
-    )
-    projected = jnp.einsum("rc,dc->rd", mixed_rows, w_out, preferred_element_type=jnp.float32)
+    mixed_own = mixed_h.reshape(seq_rows, own_q)
+    projected = multiply_scatter(
+        n_seq,
+        mixed_own.reshape((n_seq,) + part_shape[:2] + (own_q,)),
+        w_heads,
+        own_width,
+        5,
+        "project",
+    ).reshape(row_count, feat_width)
     inverse_one = scale_rows(projected)
     middle = tok_rows + projected * inverse_one * factor[1]
     inverse_two = scale_rows(middle)
@@ -1053,14 +1233,12 @@
     dmiddle = upstream + dmid_part
     dproj, gain_one = norm_back(projected, inverse_one, factor[1], dmiddle)
     dproj_bf = dproj.astype(jnp.bfloat16)
-    dmixed = jnp.dot(dproj_bf, w_out, preferred_element_type=jnp.float32).astype(jnp.bfloat16)
-    dmixed_h = lax.all_to_all(dmixed, "seq", split_axis=1, concat_axis=0, tiled=True).reshape(
-        sequence_count, seq_rows, heads, HEAD_SIZE
-    )
-    grad_out = jnp.einsum("tr,tc->rc", dproj_bf, mixed_rows, preferred_element_type=jnp.float32)
-    grad_out = lax.psum_scatter(
-        grad_out.astype(jnp.bfloat16), AXES, scatter_dimension=0, tiled=True
-    ).astype(jnp.float32)
+    whole_dproj = gather_rows(n_seq, dproj_bf.reshape(part_shape), 6).reshape(seq_rows, feat_width)
+    dmixed_h = (
+        jnp.dot(whole_dproj, w_heads[:, own_width:], preferred_element_type=jnp.float32)
+        .astype(jnp.bfloat16)
+        .reshape(sequence_count, seq_rows, heads, HEAD_SIZE)
+    )
     dquery_h, dkey_h, dvalue_h = attend_back(
         query_h, key_h, value_h, mixed_h, totals, dmixed_h, block_rows
     )
@@ -1077,48 +1255,45 @@
     dqkv = jnp.concatenate(
         [dquery_h.reshape(seq_rows, own_q), group_sum(dkey_h), group_sum(dvalue_h)], axis=1
     )
-    dnormed_in = lax.psum_scatter(
-        jnp.einsum("rc,dc->rd", dqkv, w_qkv, preferred_element_type=jnp.float32).astype(
-            jnp.bfloat16
-        ),
-        "seq",
-        scatter_dimension=0,
-        tiled=True,
-    ).astype(jnp.float32)
-    grad_qkv = jnp.einsum("tr,tc->rc", whole_xn, dqkv, preferred_element_type=jnp.float32)
-    grad_qkv = jnp.transpose(
-        grad_qkv.astype(jnp.bfloat16).reshape(n_fsdp, n_seq, n_mlp, share, own_width),
-        (0, 2, 1, 3, 4),
-    ).reshape(feat_width, own_width)
-    grad_qkv = lax.psum_scatter(grad_qkv, ("fsdp", "mlp"), scatter_dimension=0, tiled=True)
-    grad_qkv = jnp.transpose(
-        lax.all_to_all(
-            grad_qkv.reshape(n_seq, share, own_width),
-            "seq",
-            split_axis=0,
-            concat_axis=0,
-            tiled=True,
-        ),
-        (1, 0, 2),
-    ).astype(jnp.float32)
-    attn_grad = jnp.concatenate(
+    dnormed_in = multiply_scatter(
+        n_seq,
+        dqkv.reshape((n_seq,) + part_shape[:2] + (own_width,)),
+        w_heads,
+        0,
+        7,
+        "input_gradient",
+    ).reshape(row_count, feat_width)
+    grad_heads = jnp.concatenate(
         [
-            grad_qkv[:, :, :own_q].reshape(share, query_total_width),
-            grad_qkv[:, :, own_q : own_q + own_kv].reshape(share, key_value_width),
-            grad_qkv[:, :, own_q + own_kv :].reshape(share, key_value_width),
-            grad_out,
+            jnp.einsum("tr,tc->rc", whole_xn, dqkv, preferred_element_type=jnp.float32).astype(
+                jnp.bfloat16
+            ),
+            jnp.einsum(
+                "tr,tc->rc", whole_dproj, mixed_own, preferred_element_type=jnp.float32
+            ).astype(jnp.bfloat16),
         ],
         axis=1,
     )
+    grad_heads = jnp.transpose(
+        grad_heads.reshape(n_fsdp, n_seq, n_mlp, share, all_width), (0, 2, 1, 3, 4)
+    ).reshape(feat_width, all_width)
+    grad_heads = lax.psum_scatter(grad_heads, ("fsdp", "mlp"), scatter_dimension=0, tiled=True)
     dinput_part, gain_zero = norm_back(tok_rows, inverse_in, factor[0], dnormed_in)
     input_grad = dmiddle + dinput_part
 
     gain_sums = jnp.stack([gain_zero, gain_one, gain_two, gain_three])
     gain_parts = jnp.transpose(gain_sums.reshape(4, count, feat_width // count), (1, 0, 2))
     gain_parts = jnp.pad(gain_parts, ((0, 0), (0, 4), (0, 128 - feat_width // count)))
-    norm_grad = jnp.sum(exchange(sizes, gain_parts, 1), axis=0)[
-        : norm_weight.shape[0], : norm_weight.shape[1]
-    ]
+    gain_tiles, grad_cols = exchange(
+        sizes, gain_parts, grad_heads.reshape(n_seq, share, all_width), 1
+    )
+    norm_grad = jnp.sum(gain_tiles, axis=0)[: norm_weight.shape[0], : norm_weight.shape[1]]
+    pieces, start = [], 0
+    for cut in cuts:
+        piece = grad_cols[:, :, start : start + cut // n_seq]
+        pieces.append(jnp.transpose(piece, (1, 0, 2)).reshape(share, cut))
+        start += cut // n_seq
+    attn_grad = jnp.concatenate(pieces, axis=1).astype(jnp.float32)
 
     attn_new, first_attn_new, second_attn_new = adam_update(
         attention_matrix, attn_grad, attention_first_moment, attention_second_moment, decay_rate

time: 1340 us -> 1050 us (0.78)
  waiting for transfers between devices: 641 us -> 29.6 us
  Pallas kernels: 356 us -> 711 us
  starting transfers between devices: 23.6 us -> 0.16 us
  blocking collectives: 22.3 us -> 0 us
  matrix products: 128 us -> 113 us
  local copies, waits for them, and re-layouts: 60.8 us -> 74.6 us
    pallas_call x2 -> x6, Pallas kernels: 24.7 us -> 373 us  [the longest x2 159 us: gather_rows(): pl.pallas_call(functools.partial(gather_kernel, n), name='gather_rows', o...]
    reduce_scatter x3 -> x1, waiting for transfers between devices: 160 us -> 0.02 us  [on_device(): lax.psum_scatter(grad_heads, ('fsdp', 'mlp'), scatter_dimension=0, tiled=...]
    all_gather x1, waiting for transfers between devices: 140 us -> 0.01 us  [on_device(): lax.all_gather(mlp_weight.astype(jnp.bfloat16), 'fsdp', axis=1, tiled=True)]
    reduce_scatter x1, waiting for transfers between devices: 142 us -> 29.5 us  [on_device(): lax.psum_scatter(jnp.stack([grad_gate, grad_up, grad_down]).astype(jnp.bf...]
    all_gather x3 -> x1, waiting for transfers between devices: 106 us -> 0.02 us  [on_device(): w_heads = lax.all_gather(head_cols, ('fsdp', 'mlp'), axis=0, tiled=False)]
    all_to_all x3 -> x0, waiting for transfers between devices: 92.6 us -> none  [the longest x1 48.1 us: on_device(): lax.all_to_all(mixed_h.reshape(seq_rows, own_q), 'seq', split_axis=0, con...]
    all_to_all x3 -> x0, starting transfers between devices: 23.3 us -> none  [the longest x1 14.7 us: on_device(): lax.all_to_all(mixed_h.reshape(seq_rows, own_q), 'seq', split_axis=0, con...]
    all_to_all x1 -> x0, blocking collectives: 22.3 us -> none  [on_device(): lax.all_to_all(jnp.transpose(head_parts, (1, 0, 2)), 'seq', split_axis=0,...]
  transfers between devices with their start and end apart: 11 -> 4, of which waited for: 10 -> 1; matrix products, arithmetic and copies ran while one was open for 11% -> 13% of each run, Pallas kernels for 2% -> 26%
where the time goes in v2:
time: 1050 us; the launch traced here: 1040 us
  Pallas kernels  711 us (68%)
  matrix products  113 us (11%)
  other arithmetic  92.3 us (9%)
  local copies, waits for them, and re-layouts  74.6 us (7%)
  waiting for transfers between devices  29.6 us (3%)
  between operations  15.1 us (1%)
    pallas_call x2, Pallas kernels, mlp_half(): pl.pallas_call(kernel, name='mlp_forward' if forward else 'mlp_backward',...  337 us
    pallas_call x2, Pallas kernels, gather_rows(): pl.pallas_call(functools.partial(gather_kernel, n), name='gather_rows', o...  159 us
    pallas_call x2, Pallas kernels, multiply_scatter(): pl.pallas_call(functools.partial(multiply_scatter_kernel, n, first), name...  158 us
    pallas_call x2, Pallas kernels, exchange(): pl.pallas_call(functools.partial(exchange_kernel, sizes), name='exchange'...  56 us
    reduce_scatter x1, waiting for transfers between devices, on_device(): lax.psum_scatter(jnp.stack([grad_gate, grad_up, grad_down]).astype(jnp.bf...  29.5 us
    sub x3, other arithmetic, adam_update(): weight - learn_rate * (first_hat / (jnp.sqrt(second_hat) + adam_eps) + de...  24.4 us
  transfers between devices with their start and end apart: 4, of which 1 were waited for; matrix products, arithmetic and copies ran while one was open for 13% of the time, Pallas kernels for 26%

profile of v2, /device:TPU:0, one launch (start us, length us, event | category | flops | bytes accessed | tf_op | source)
XLA Modules:
  0.0 1035.8 jit_solution(4854806439973002493)
XLA Ops:
  7.2 1.6 convert_element_type.165
  10.6 28.5 %exchange.2 = (f32[32,8,128]{2,1,0:T(8,128)}, bf16[4,72,1536]{2,1,0:T(8,128)(2,1)}) custom-call(f32[1,8,128]{2,1,0:T(8,128)} %pad_convert_fusion.mine_ref, bf16[4,72,1536]{2,1,0:T(8,128)(2,1)} %maximum_bitcast_fusion.block_ref), custom_call_target="tpu_custom_call" | custom-call | tf_op jit(solution)/shard_map/exchange/pallas_call | solution.py:423
  39.1 5.6 convert_element_type.169
  47.8 1.3 multiply_convert_fusion.3.own
  49.1 85.7 %gather_rows.2 = bf16[4,2,128,2304]{3,2,1,0:T(8,128)(2,1)} custom-call(bf16[2,128,2304]{2,1,0:T(8,128)(2,1)} %multiply_convert_fusion.3.own), custom_call_target="tpu_custom_call" | custom-call | tf_op jit(solution)/shard_map/gather_rows/pallas_call | solution.py:998
  135.2 3.9 copy.98
  139.1 10.2 fusion.90
  152.5 1.5 copy.99
  155.0 11.0 %while.39 = (s32[]{:T(128)}, bf16[1,1024,2,256]{3,1,2,0:T(8,128)(2,1)}, f32[1,2,1024]{2,1,0:T(2,128)S(1)}, bf16[1,1024,2,256]{3,1,2,0:T(8,128)(2,1)S(1)}, bf16[1...) while((s32[]{:T(128)}, ...), condition=%wide.region_3.0_spmd.clone, body=%wide.region_1.3_spmd.clone.sunk | while | flops 1083964928 | bytes 14184639 | solution.py:89
  155.4 3.0 select_reduce_fusion.2
  158.4 2.1 fusion.136
  161.0 2.9 select_reduce_fusion.2
  163.9 2.1 fusion.136
  166.0 3.3 copy.102
  169.3 2.3 copy.112
  171.6 2.5 reshape_reshape.3.left
  174.1 82.5 %project.1 = f32[2,128,2304]{2,1,0:T(8,128)} custom-call(bf16[4,2,128,512]{3,2,1,0:T(8,128)(2,1)} %reshape_reshape.3.left, bf16[2304,1536]{1,0:T(8,128)(2,1)} %bitcast.296), custom_call_target="tpu_custom_call" | custom-call | tf_op jit(solution)/shard_map/project/pallas_call | solution.py:1088
  256.5 2.1 multiply_reduce_fusion.8
  259.7 4.0 multiply_convert_fusion.2
  263.7 12.1 %slice_bitcast_fusion = (bf16[2304,1152]{1,0:T(8,128)(2,1)}, bf16[2304,1152]{1,0:T(8,128)(2,1)}, bf16[2304,1152]{1,0:T(8,128)(2,1)}) fusion(bf16[3,2304,1152]{2,1,0:T(8,128)(2,1)} %all-gather.4.cloned.1.call-done), kind=kLoop, calls=%fused_computation.75 | loop fusion | bytes 31850496 | tf_op jit(solution)/shard_map/squeeze | solution.py:1195
  275.8 171.9 %mlp_forward.1 = (bf16[4,8,64,2304]{3,2,1,0:T(8,128)(2,1)}, bf16[4,512,1152]{2,1,0:T(8,128)(2,1)}, bf16[4,512,1152]{2,1,0:T(8,128)(2,1)}, bf16[4,512,1152]{2,1,0:T(8,128)(2,1)}, f32[4,64,2304]{2,1,0:T(8,128)}) custom-call(bf16[4,64,2304]{2,1,0:T(8,128)(2,1)} %get-tuple-element.633.refs_0_, bf16[2304,1152]{1,0:T(8,128)(2,1)} %get-tuple-element.639.refs_1_, ...), custom_call_target="tpu_custom_call" | custom-call | flops 32614907904 | bytes 15925248 | tf_op jit(solution)/shard_map/mlp_forward/pallas_call | solution.py:933
  447.7 1.9 multiply_reduce_fusion.6
  449.7 3.6 fusion.79
  453.4 3.9 multiply_convert_fusion.1.refs_0_
  457.3 165.3 %mlp_backward.1 = (bf16[4,8,64,2304]{3,2,1,0:T(8,128)(2,1)}, bf16[4,512,1152]{2,1,0:T(8,128)(2,1)}, bf16[4,512,1152]{2,1,0:T(8,128)(2,1)}, f32[4,64,2304]{2,1,0:T(8,128)}) custom-call(bf16[4,64,2304]{2,1,0:T(8,128)(2,1)} %multiply_convert_fusion.1.refs_0_, bf16[2304,1152]{1,0:T(8,128)(2,1)} %get-tuple-element.639.refs_1_, ...), custom_call_target="tpu_custom_call" | custom-call | flops 32614907904 | bytes 15925248 | tf_op jit(solution)/shard_map/mlp_backward/pallas_call | solution.py:933
  622.7 3.5 multiply_reduce_fusion
  626.4 5.2 multiply_reduce_fusion.1
  631.6 2.4 fusion.73.own
  634.0 73.5 %gather_rows.3 = bf16[4,2,128,2304]{3,2,1,0:T(8,128)(2,1)} custom-call(bf16[2,128,2304]{2,1,0:T(8,128)(2,1)} %fusion.73.own), custom_call_target="tpu_custom_call" | custom-call | tf_op jit(solution)/shard_map/gather_rows/pallas_call | solution.py:998
  707.5 6.7 fusion.94
  714.2 2.4 copy.105
  716.6 1.9 multiply_reduce_fusion.9
  719.5 34.1 %while.40 = (s32[]{:T(128)}, bf16[1,1024,2,256]{3,1,2,0:T(8,128)(2,1)}, f32[1,1024,2,256]{1,3,2,0:T(8,128)S(1)}, f32[1,1024,2,256]{1,3,2,0:T(8,128)}, bf16[1,102...) while((s32[]{:T(128)}, ...), condition=%wide.region_12.13_spmd.clone, body=%wide.region_11.12_spmd.clone.sunk | while | flops 2704015872 | bytes 100172312 | solution.py:133
  719.5 1.9 fusion.147
  721.9 1.6 copy-done.4
  723.6 3.5 multiply_convert_fusion.5
  727.2 2.8 bitcast_add_fusion.5
  732.6 3.2 bitcast_add_fusion.6
  735.8 1.9 fusion.147
  738.2 1.6 copy-done.4
  739.9 3.5 multiply_convert_fusion.5
  743.5 2.8 bitcast_add_fusion.5
  748.9 4.8 bitcast_add_fusion.6
  753.7 2.3 copy.111
  756.0 2.0 convert_reduce_fusion
  758.2 6.6 convolution_convert_fusion.5
  764.8 6.7 convolution_convert_fusion.4
  771.5 5.1 pad_maximum_fusion.1
  776.6 10.3 copy.113
  786.8 6.7 copy.114
  793.6 16.4 %fusion.53 = bf16[1,2304,1152]{2,1,0:T(8,128)(2,1)S(1)} fusion(bf16[2048,2304]{1,0:T(8,128)(2,1)} %bitcast.330, bf16[2048,1152]{1,0:T(8,128)(2,1)} %bitcast.339), kind=kOutput, calls=%fused_computation.67 | convolution fusion | flops 10874290176 | bytes 19464192 | tf_op jit(solution)/shard_map/rd,rf->df/dot_general | solution.py:1219
  810.1 15.2 %fusion.54 = bf16[1,2304,1152]{2,1,0:T(8,128)(2,1)S(1)} fusion(bf16[2048,2304]{1,0:T(8,128)(2,1)S(1)} %bitcast.333, bf16[2048,1152]{1,0:T(8,128)(2,1)} %bitcast.338), kind=kOutput, calls=%fused_computation.68 | convolution fusion | flops 10874290176 | bytes 19464192 | tf_op jit(solution)/shard_map/rd,rf->df/dot_general | solution.py:1220
  825.3 15.3 %fusion.55 = bf16[1,2304,1152]{2,1,0:T(8,128)(2,1)S(1)} fusion(bf16[2048,2304]{1,0:T(8,128)(2,1)} %bitcast.334, bf16[2048,1152]{1,0:T(8,128)(2,1)S(1)} %bitcast.337), kind=kOutput, calls=%fused_computation.69 | convolution fusion | flops 10874290176 | bytes 19464192 | tf_op jit(solution)/shard_map/rd,rf->df/dot_general | solution.py:1223
  840.6 7.1 pad_maximum_fusion
  847.7 1.2 copy-done.16
  853.1 1.6 pad_maximum_fusion.2.left
  854.7 75.8 %input_gradient.1 = f32[2,128,2304]{2,1,0:T(8,128)} custom-call(bf16[4,2,128,1024]{3,2,1,0:T(8,128)(2,1)} %pad_maximum_fusion.2.left, bf16[2304,1536]{1,0:T(8,128)(2,1)} %bitcast.298), custom_call_target="tpu_custom_call" | custom-call | tf_op jit(solution)/shard_map/input_gradient/pallas_call | solution.py:1088
  930.6 2.3 multiply_reduce_fusion.2
  934.2 7.3 fusion.63
  941.6 27.5 %exchange.3 = (f32[32,8,128]{2,1,0:T(8,128)}, bf16[4,72,1536]{2,1,0:T(8,128)(2,1)}) custom-call(f32[32,8,128]{2,1,0:T(8,128)} %pad.10.mine_ref, bf16[4,72,1536]{2,1,0:T(8,128)(2,1)} %bitcast.324), custom_call_target="tpu_custom_call" | custom-call | tf_op jit(solution)/shard_map/exchange/pallas_call | solution.py:423
  969.1 1.1 slice_bitcast_fusion.4
  975.6 5.1 multiply_subtract_fusion.1
  980.7 29.5 %reduce-scatter.5.cloned.1.call-done = bf16[3,576,1152]{2,1,0:T(8,128)(2,1)} async-done(((bf16[3,2304,1152]{2,1,0:T(8,128)(2,1)}), bf16[3,576,1152]{2,1,0:T(8,128)(2,1)}) %reduce-scatter.5.cloned.1.call-update) | async-done | bytes 3981328 | tf_op jit(solution)/shard_map/reduce_scatter | solution.py:1226
  1010.2 18.7 %multiply_subtract_fusion = (f32[3,576,1152]{2,1,0:T(8,128)}, f32[3,576,1152]{2,1,0:T(8,128)}, f32[3,576,1152]{2,1,0:T(8,128)}, f32[3,576,1152]{2,1,0:T(8,128)}) fusion(f32[3,576,1152]{2,1,0:T(8,128)} %param.22, f32[3,576,1152]{2,1,0:T(8,128)} %param.23, f32[3,576,1152]{2,1,0:T(8,128)} %param.24, bf16[3,576,1152]{2,1,0:T(8,128)(2,1)} %reduce-scatter.5.cloned.1.call-done), kind=kLoop, calls=%fused_computation.71 | loop fusion | flops 31850496 | bytes 59719680 | tf_op jit(solution)/shard_map/sub | solution.py:50
  (239 shorter events, 30.0 us)
Async XLA Ops:
  7.2 128.0 %all-gather.6.cloned.1.call-start = ((), (), s32[]{:S(2)}) async-start(), calls=%async_computation.5 | async-start | bytes 7962624 | tf_op jit(solution)/shard_map/all_gather | solution.py:1156
  39.1 224.6 %all-gather.4.cloned.1.call-start = ((), (), s32[]{:S(2)}) async-start(), calls=%async_computation.2 | async-start | bytes 19906560 | tf_op jit(solution)/shard_map/all_gather | solution.py:1194
  44.8 896.8 %reduce-scatter.3.cloned.1.call-start = ((), (), s32[]{:S(2)}) async-start(), calls=%async_computation.3 | async-start | bytes 7962624 | tf_op jit(solution)/shard_map/reduce_scatter | solution.py:1280
  46.5 2.7 copy-start.35
  134.9 496.7 %copy-start.31 = (f32[2304]{0:T(1024)}, f32[2304]{0:T(1024)S(1)}, u32[]{:S(2)}) copy-start(f32[2304]{0:T(1024)S(1)} %mul.582) | copy-start | bytes 27652
  135.0 496.6 %copy-start.33 = (f32[2304]{0:T(1024)}, f32[2304]{0:T(1024)S(1)}, u32[]{:S(2)}) copy-start(f32[2304]{0:T(1024)S(1)} %mul.596) | copy-start | bytes 27652
  135.1 318.3 %copy-start.37 = (f32[2304]{0:T(1024)}, f32[2304]{0:T(1024)S(1)}, u32[]{:S(2)}) copy-start(f32[2304]{0:T(1024)S(1)} %mul.602) | copy-start | bytes 27652
  139.1 10.3 copy-start.7
  155.4 3.1 copy-start.29
  161.0 2.9 copy-start.29
  258.6 367.8 %copy-start.43 = (f32[256]{0:T(256)}, f32[256]{0:T(256)S(1)}, u32[]{:S(2)}) copy-start(f32[256]{0:T(256)S(1)} %get-tuple-element.657) | copy-start | bytes 3076
  259.5 366.9 %copy-start.45 = (f32[256]{0:T(256)}, f32[256]{0:T(256)S(1)}, u32[]{:S(2)}) copy-start(f32[256]{0:T(256)S(1)} %get-tuple-element.655) | copy-start | bytes 3076
  449.7 3.6 copy-start.49
  626.3 5.3 copy-start.51
  626.4 5.2 copy-start.3
  626.4 5.2 copy-start.8
  626.4 5.2 copy-start.10
  714.2 5.3 copy-start.6
  719.5 4.1 copy-start.18
  719.5 4.1 copy-start.30
  727.2 2.8 copy-start.9
  727.2 2.8 copy-start.11
  727.2 2.9 copy-start.14
  727.2 4.5 copy-start.13
  727.2 4.5 copy-start.19
  730.0 2.6 copy-start.5
  735.8 4.1 copy-start.18
  735.8 4.1 copy-start.30
  743.4 2.8 copy-start.9
  743.5 2.8 copy-start.11
  743.5 2.9 copy-start.14
  743.5 4.5 copy-start.13
  743.5 4.5 copy-start.19
  746.3 2.6 copy-start.5
  755.9 8.8 slice-start
  757.9 6.8 copy-start.20
  758.1 6.6 copy-start.22
  758.1 6.6 slice-start.1
  758.1 6.6 copy-start.28
  793.5 16.5 %slice-start.2 = ((s8[9437184]{0:T(1024)(128)(4,1)}), s8[1048576]{0:T(1024)(128)(4,1)S(1)}, s32[]{:S(2)}) async-start(s8[9437184]{0:T(1024)(128)(4,1)} %bitcast.331), calls=%async_computation.8 | async-start | bytes 2097152
  793.6 216.6 %reduce-scatter.5.cloned.1.call-start = ((), (), s32[]{:S(2)}) async-start(), calls=%async_computation.4 | async-start | bytes 19906560 | tf_op jit(solution)/shard_map/reduce_scatter | solution.py:1226
  793.6 16.4 %slice-start.3 = ((s8[9437184]{0:T(1024)(128)(4,1)}), s8[4194304]{0:T(1024)(128)(4,1)S(1)}, s32[]{:S(2)}) async-start(s8[9437184]{0:T(1024)(128)(4,1)} %bitcast.331), calls=%async_computation.9 | async-start | bytes 8388608
  793.6 16.4 %slice-start.4 = ((s8[9437184]{0:T(1024)(128)(4,1)}), s8[4194304]{0:T(1024)(128)(4,1)S(1)}, s32[]{:S(2)}) async-start(s8[9437184]{0:T(1024)(128)(4,1)} %bitcast.331), calls=%async_computation.10 | async-start | bytes 8388608
  793.6 31.6 %slice-start.5 = ((s8[4718592]{0:T(1024)(128)(4,1)}), s8[4194304]{0:T(1024)(128)(4,1)S(1)}, s32[]{:S(2)}) async-start(s8[4718592]{0:T(1024)(128)(4,1)} %bitcast.335), calls=%async_computation.11 | async-start | bytes 8388608
  810.1 15.2 %slice-start.6 = ((s8[4718592]{0:T(1024)(128)(4,1)}), s8[524288]{0:T(1024)(128)(4,1)S(1)}, s32[]{:S(2)}) async-start(s8[4718592]{0:T(1024)(128)(4,1)} %bitcast.335), calls=%async_computation.12 | async-start | bytes 1048576
  854.7 75.8 %copy-start.1 = (f32[1,256,2304]{2,1,0:T(8,128)S(1)}, f32[1,256,2304]{2,1,0:T(8,128)}, u32[]{:S(2)}) copy-start(f32[1,256,2304]{2,1,0:T(8,128)} %param.17) | copy-start | bytes 7077892
  854.7 75.8 %copy-start.36 = (f32[2304]{0:T(1024)S(1)}, f32[2304]{0:T(1024)}, u32[]{:S(2)}) copy-start(f32[2304]{0:T(1024)} %copy-done.35) | copy-start | bytes 27652
  854.7 75.8 %copy-start.48 = (f32[2,128]{1,0:T(2,128)S(1)}, f32[2,128]{1,0:T(2,128)}, u32[]{:S(2)}) copy-start(f32[2,128]{1,0:T(2,128)} %copy-done.47) | copy-start | bytes 3076
  930.5 2.5 copy-start.41
  930.5 2.6 copy-start.40
  930.6 2.7 copy-start.39
  930.6 3.6 copy-start.32
  930.6 3.6 copy-start.34
  930.6 3.6 copy-start.38
  930.6 3.6 copy-start.44
  930.6 3.6 copy-start.46
  930.6 3.6 copy-start.50
  930.6 3.6 copy-start.52
  930.6 3.6 copy-start.55
  941.5 33.5 %copy-start.54 = (f32[4,72]{1,0:T(4,128)S(1)}, f32[4,72]{1,0:T(4,128)}, u32[]{:S(2)}) copy-start(f32[4,72]{1,0:T(4,128)} %param.25) | copy-start | bytes 3460
  941.5 33.5 %copy-start.56 = (f32[4,72]{1,0:T(4,128)S(1)}, f32[4,72]{1,0:T(4,128)}, u32[]{:S(2)}) copy-start(f32[4,72]{1,0:T(4,128)} %param.26) | copy-start | bytes 3460
  941.5 33.5 %copy-start.57 = (f32[4,72]{1,0:T(4,128)S(1)}, f32[4,72]{1,0:T(4,128)}, u32[]{:S(2)}) copy-start(f32[4,72]{1,0:T(4,128)} %param.27) | copy-start | bytes 3460
  941.5 34.1 %copy-start.17 = (f32[72,6144]{1,0:T(8,128)S(1)}, f32[72,6144]{1,0:T(8,128)}, u32[]{:S(2)}) copy-start(f32[72,6144]{1,0:T(8,128)} %param.19) | copy-start | bytes 5308420
  941.5 34.1 %copy-start.26 = (f32[72,6144]{1,0:T(8,128)S(1)}, f32[72,6144]{1,0:T(8,128)}, u32[]{:S(2)}) copy-start(f32[72,6144]{1,0:T(8,128)} %param.20) | copy-start | bytes 5308420
  (17 other events, 26.1 us)
Sparse Core Ops, SparseCore 0:
  39.2 51.7 all-gather.5
  93.4 150.1 all-gather.3
  793.7 64.8 reduce-scatter.2
  861.5 148.6 reduce-scatter.4
